TPU v7x, 128 devices: a whole 4x4x4 slice. The times are simulated.
128 devices in a mesh: cells: 32 (over y, x, core), vecs: 4 (over z).
Axes of the slice: x: 4, y: 4, z: 4, core: 2. Of those that a mesh axis runs over, the one named last changes fastest.
Arguments:
- vectors: float32 [64, 32, 64, 128], P(None, 'cells', 'vecs'), may hold values from -120 to 120
- potential: float32 [64, 32, 128], P(None, 'cells'), may hold values from -0.5 to 0.5
- hopping: float32 [27, 64, 64], replicated, may hold values from -0.07 to 0.07
- center: float32 [1], replicated, may hold values from -0.3 to 0.3
Outputs:
- filtered: float32 [64, 32, 64, 128], P(None, 'cells', 'vecs')
All inputs are finite; a program needn't handle non-finite values.
Results may differ from a plain program's by a relative error of at most 0.0003.
Values sent between devices are 32-bit elements; how exact they have to be, the bound alone decides.
No kernel may reach another device: no remote copies, remote signals or barrier semaphores. Data moves between devices by JAX's collectives and lax.ppermute only.
A program may use at most 128 MiB of HBM per device.

v0:
```python
import math

import jax
import jax.numpy as jnp
from jax import lax
from jax.experimental import pallas as pl
from jax.experimental.pallas import tpu as pltpu
from jax.sharding import Mesh, PartitionSpec as P


ORB = 64
NVEC = 64
NY = 16
NZ = 8
CELLS = NY * NZ
STEPS = 4
HALF = 8
F32 = jnp.float32
BF16 = jnp.bfloat16


LIMIT = pltpu.CompilerParams(vmem_limit_bytes=8 * 1024 * 1024)


def split(x):
    high = x.astype(BF16)
    return high, (x - high.astype(F32)).astype(BF16)


def halves_body(vectors, *refs):
    copies = [
        pltpu.make_async_copy(vectors.at[:, h * HALF : (h + 1) * HALF], refs[h], refs[2 + h])
        for h in range(2)
    ]
    for copy in copies:
        copy.start()
    for copy in copies:
        copy.wait()


def split_halves(vectors):
    vmem = pl.BlockSpec(memory_space=pltpu.VMEM)
    return pl.pallas_call(
        halves_body,
        in_specs=[pl.BlockSpec(memory_space=pl.ANY)],
        out_specs=[vmem, vmem],
        out_shape=[jax.ShapeDtypeStruct((ORB, HALF, CELLS), F32)] * 2,
        scratch_shapes=[pltpu.SemaphoreType.DMA, pltpu.SemaphoreType.DMA],
        compiler_params=LIMIT,
    )(vectors)


def weights_body(order, hop, out):
    for iz in range(3):
        parts = []
        for iy in range(3):
            for ix in range(3):
                d = 9 * order[ix] + 3 * iy + iz
                parts.append(0.5 * (hop[d] + jnp.transpose(hop[26 - d])))
        high, low = split(jnp.concatenate(parts, axis=1))
        high = high.astype(F32)
        whole = jnp.concatenate([high, high, low.astype(F32)], axis=1)
        out[iz * ORB : (iz + 1) * ORB, :] = whole.astype(BF16)


def weights(order, hopping):
    return pl.pallas_call(
        weights_body,
        in_specs=[pl.BlockSpec(memory_space=pltpu.SMEM), pl.BlockSpec(memory_space=pltpu.VMEM)],
        out_shape=jax.ShapeDtypeStruct((3 * ORB, 27 * ORB), BF16),
        compiler_params=LIMIT,
    )(order, hopping)


def step_body(first, *refs):
    if first:
        center, pot, w, cur, left, right, out = refs
    else:
        center, pot, w, cur, left, right, prev, out = refs
    onsite = pot[...] - center[0]
    lane = lax.broadcasted_iota(jnp.int32, (ORB, CELLS), 1) % NZ
    for pair in range(HALF // 2):
        rows = [pl.ds(2 * pair + i, ORB, stride=HALF) for i in range(2)]
        own = [cur[r, :] for r in rows]
        columns = []
        for i in range(2):
            here = jnp.concatenate([left[rows[i], :], own[i], right[rows[i], :]], axis=0)
            below, above = pltpu.roll(here, NZ, 1), pltpu.roll(here, CELLS - NZ, 1)
            columns.append(jnp.concatenate([below, here, above], axis=0))
        high, low = split(jnp.concatenate(columns, axis=1))
        stacked = jnp.concatenate([high, low, high], axis=0)
        product = jnp.dot(w[...], stacked, preferred_element_type=F32)
        for i in range(2):
            below, here, above = (
                product[iz * ORB : (iz + 1) * ORB, i * CELLS : (i + 1) * CELLS] for iz in range(3)
            )
            below = jnp.where(
                lane == 0, pltpu.roll(below, CELLS - NZ + 1, 1), pltpu.roll(below, 1, 1)
            )
            above = jnp.where(
                lane == NZ - 1, pltpu.roll(above, NZ - 1, 1), pltpu.roll(above, CELLS - 1, 1)
            )
            total = onsite * own[i] + here + below + above
            if not first:
                total = 2.0 * total - prev[rows[i], :]
            out[rows[i], :] = total


def apply_step(center, pot, w, cur, left, right, prev=None):
    first = prev is None
    vmem = pl.BlockSpec(memory_space=pltpu.VMEM)
    args = (center, pot, w, cur, left, right) + (() if first else (prev,))
    return pl.pallas_call(
        lambda *refs: step_body(first, *refs),
        in_specs=[pl.BlockSpec(memory_space=pltpu.SMEM)] + [vmem] * (len(args) - 1),
        out_specs=vmem,
        out_shape=jax.ShapeDtypeStruct((ORB * HALF, CELLS), F32),
        compiler_params=LIMIT,
    )(*args)


def changed_over(x, flag, axis):
    quarters = jnp.split(x, 4, axis=axis)
    return jnp.where(flag[0] == 1, jnp.concatenate([quarters[i] for i in (0, 3, 2, 1)], axis), x)


def gram_body(flag, *refs):
    pieces, out = refs[:-1], refs[-1]
    total = jnp.zeros((NVEC, 2 * NVEC), F32)
    for o in range(0, ORB, 2):
        rows = jnp.concatenate(
            [
                jnp.concatenate([p[(o + i) * HALF : (o + i + 1) * HALF, :] for p in pieces], axis=0)
                for i in range(2)
            ],
            axis=1,
        )
        high, low = split(rows)
        both = jnp.concatenate([high, low], axis=0)
        total = total + lax.dot_general(
            high, both, (((1,), (1,)), ((), ())), preferred_element_type=F32
        )
    cross = total[:, NVEC:]
    gram = total[:, :NVEC] + cross + jnp.transpose(cross)
    gram = changed_over(changed_over(gram, flag, 0), flag, 1)
    q = NVEC // 4
    out[: q, :] = jnp.concatenate(
        [gram[:q], gram[q : 2 * q, q:], gram[3 * q :, 3 * q :]], axis=1
    )
    row = gram[2 * q : 3 * q, 2 * q :]
    pad = jnp.zeros((q // 2, 2 * NVEC - 4 * q), F32)
    out[q:, :] = jnp.concatenate([row[: q // 2], row[q // 2 :], pad], axis=1)


def gram_of(flag, pieces):
    vmem = pl.BlockSpec(memory_space=pltpu.VMEM)
    return pl.pallas_call(
        gram_body,
        in_specs=[pl.BlockSpec(memory_space=pltpu.SMEM)] + [vmem] * len(pieces),
        out_shape=jax.ShapeDtypeStruct((3 * NVEC // 8, 2 * NVEC), F32),
        compiler_params=LIMIT,
    )(flag, *pieces)


def mix_body(factor, flag, copies, *refs):
    pieces, out = refs[:-1], refs[-1]
    packed = jnp.sum(copies[...], axis=0)
    q = NVEC // 4
    row = lax.broadcasted_iota(jnp.int32, packed.shape, 0)
    at = lax.broadcasted_iota(jnp.int32, packed.shape, 1)
    upper = jnp.where((at < q) | ((at >= 4 * q) & (at < 5 * q)) | (at >= 7 * q), 1.0, 2.0)
    lower = jnp.where(at % (2 * q) < q, 1.0, 2.0)
    weighted = packed * packed * jnp.where(row < q, upper, lower)
    squares = jnp.sum(jnp.sum(weighted, axis=1, keepdims=True), axis=0, keepdims=True)
    frobenius = jnp.sqrt(squares)
    mine = packed[:q, :NVEC]
    rows = lax.broadcasted_iota(jnp.int32, mine.shape, 0)
    cols = lax.broadcasted_iota(jnp.int32, mine.shape, 1)
    eye = jnp.where(rows == cols, 1.0, 0.0).astype(F32)
    mixing = (1.5 * eye - 0.5 * mine / frobenius) * (factor / jnp.sqrt(frobenius))
    mixing = changed_over(mixing, flag, 1)
    tall = jnp.concatenate([mixing] * 4, axis=0)
    wide = jnp.concatenate([tall] * 4, axis=1)
    rows = lax.broadcasted_iota(jnp.int32, wide.shape, 0) // (2 * HALF)
    cols = lax.broadcasted_iota(jnp.int32, wide.shape, 1) // NVEC
    wide = jnp.where(rows == cols, wide, 0.0)
    high, low = split(wide)
    high_lhs = high
    both_lhs = jnp.concatenate([high, low], axis=0)
    for group in range(ORB // 8):
        halves = []
        for side in range(2):
            at = group * 8 + side * 4
            halves.append(
                jnp.concatenate(
                    [
                        p[(at + i) * HALF : (at + i + 1) * HALF, :]
                        for i in range(4)
                        for p in pieces
                    ],
                    axis=0,
                )
            )
        data = jnp.concatenate(halves, axis=1)
        high, low = split(data)
        both = jnp.dot(both_lhs, high, preferred_element_type=F32)
        mixed = jnp.dot(high_lhs, low, preferred_element_type=F32)
        mixed = mixed + both[: 8 * HALF] + both[8 * HALF :]
        for side in range(2):
            at = (group * 8 + side * 4) * 2 * HALF
            out[at : at + 8 * HALF, :] = mixed[:, side * CELLS : (side + 1) * CELLS]


def mix(factor, flag, copies, pieces):
    vmem = pl.BlockSpec(memory_space=pltpu.VMEM)
    return pl.pallas_call(
        lambda *refs: mix_body(factor, *refs),
        in_specs=[pl.BlockSpec(memory_space=pltpu.SMEM)] + [vmem] * (1 + len(pieces)),
        out_shape=jax.ShapeDtypeStruct((ORB * 2 * HALF, CELLS), F32),
        compiler_params=LIMIT,
    )(flag, copies, *pieces)


def filtered(vectors, potential, hopping, center):
    cells = ("chip", "core")
    count = lax.axis_size("chip") * lax.axis_size("core")
    ring = lax.axis_size("vecs")
    outer = [(i, (i + 1) % count if i % 2 else (i - 1) % count) for i in range(count)]
    inner = [(0, 1), (1, 0)]
    flips = ((1, 3), (3, 1))
    early, late = (
        [(k * ring + i, k * ring + (i ^ flips[k][turn])) for k in range(2) for i in range(ring)]
        for turn in range(2)
    )
    pot = potential.reshape(ORB, CELLS)
    halves = [h.reshape(ORB * HALF, CELLS) for h in split_halves(vectors.reshape(ORB, -1, CELLS))]
    core = lax.axis_index("core")
    order = jnp.stack([2 * core, jnp.ones_like(core), 2 - 2 * core]).astype(jnp.int32)
    w = weights(order, hopping)
    prev = [None, None]
    cur = halves
    for _ in range(STEPS):
        following = []
        for h in range(2):
            away = lax.ppermute(cur[h], cells, outer)
            beside = lax.ppermute(cur[h], "core", inner)
            following.append(apply_step(center, pot, w, cur[h], away, beside, prev[h]))
        prev, cur = cur, following
    a, b = cur
    planes = ("core", "vecs")
    a_early = lax.ppermute(a, planes, early)
    a_late = lax.ppermute(a, planes, late)
    b_early = lax.ppermute(b, planes, early)
    b_late = lax.ppermute(b, planes, late)
    a_far = lax.ppermute(a_early, planes, late)
    b_far = lax.ppermute(b_early, planes, late)
    pieces = (a, b, a_early, b_early, a_far, b_far, a_late, b_late)
    flag = core.reshape(1).astype(jnp.int32)
    gram = gram_of(flag, pieces)
    gram = gram + lax.ppermute(gram, "core", [(0, 1), (1, 0)])
    chips = lax.axis_size("chip")
    copies = lax.all_to_all(
        jnp.broadcast_to(gram, (chips, *gram.shape)), "chip", split_axis=0, concat_axis=0, tiled=True
    )
    factor = math.sqrt(float(count * CELLS))
    out = mix(factor, flag, copies, pieces)
    return out.reshape(ORB, 1, 2 * HALF, CELLS)


def solution(mesh):
    cells, vecs = mesh.shape["cells"], mesh.shape["vecs"]
    fine = Mesh(mesh.devices.reshape(cells // 2, 2, vecs), ("chip", "core", "vecs"))
    both = ("chip", "core")
    placed = (P(None, both, "vecs", None), P(None, both, None), P(), P())
    return jax.shard_map(
        filtered,
        mesh=fine,
        in_specs=placed,
        out_specs=P(None, both, "vecs", None),
        check_vma=False,
    )
```

profile of v0, /device:TPU:0, one launch (start us, length us, event | category | flops | bytes accessed | tf_op | source)
XLA Modules:
  0.0 83.5 jit_solution(10923107144780541096)
XLA Ops:
  1.1 4.8 %collective-permute-start = (f32[512,128]{1,0:T(8,128)S(1)}, f32[512,128]{1,0:T(8,128)S(1)}, u32[]{:S(2)}, u32[]{:S(2)}) collective-permute-start(f32[512,128]{1,0:T(8,128)S(1)} %bitcast.22), channel_id=1, source_target_pairs={{0,124},{4,8},{8,4},{12,16},{16,12},{20,24},{24,20},{28,32},{32,28... | collective-permute-start | bytes 786440 | tf_op jit(solution)/shard_map/ppermute | solution.py:245
  11.6 4.8 %collective-permute-start.2 = (f32[512,128]{1,0:T(8,128)S(1)}, f32[512,128]{1,0:T(8,128)S(1)}, u32[]{:S(2)}, u32[]{:S(2)}) collective-permute-start(f32[512,128]{1,0:T(8,128)S(1)} %shard_map.48.refs_3_.refs_6_), channel_id=1, source_target_pairs={{0,124},{4,8},{8,4},{12,16},{16,12},{20,24},{24,20},{28,32},{32,28... | collective-permute-start | bytes 786440 | tf_op jit(solution)/shard_map/ppermute | solution.py:245
  17.7 1.5 %collective-permute-start.10 = (f32[512,128]{1,0:T(8,128)S(1)}, f32[512,128]{1,0:T(8,128)S(1)}, u32[]{:S(2)}, u32[]{:S(2)}) collective-permute-start(f32[512,128]{1,0:T(8,128)S(1)} %shard_map.52.refs_3_.refs_6_), channel_id=1, source_target_pairs={{0,124},{4,8},{8,4},{12,16},{16,12},{20,24},{24,20},{28,32},{32,28... | collective-permute-start | bytes 786440 | tf_op jit(solution)/shard_map/ppermute | solution.py:245
  19.3 1.5 %collective-permute-done.2.refs_4_ = f32[512,128]{1,0:T(8,128)S(1)} collective-permute-done((f32[512,128]{1,0:T(8,128)S(1)}, f32[512,128]{1,0:T(8,128)S(1)}, u32[]{:S(2)}, u32[]{:S(2)}) %collective-permute-start.2) | collective-permute-done | bytes 262176 | tf_op jit(solution)/shard_map/ppermute | solution.py:245
  20.8 1.3 %shard_map.49.refs_3_.refs_6_ = f32[512,128]{1,0:T(8,128)S(1)} custom-call(f32[1]{0:T(128)S(6)} %copy.6.refs_0_, f32[64,128]{1,0:T(8,128)S(1)} %bitcast.12, bf16[192,1728]{1,0:T(8,128)(2,1)S(1)} %shard_map.46.refs_2_, f32[512,128]{1,0:T(8,128)S(1)} %shard_map.48.refs_3_.refs_6_, f32[512,128]{1,0:T(8,128)S(1)} %collective-permute-done.2.refs_4_, ...), custom_call_target="tpu_custom_call" | custom-call | tf_op jit(solution)/shard_map/pallas_call | solution.py:113
  22.1 4.8 %collective-permute-start.4 = (f32[512,128]{1,0:T(8,128)S(1)}, f32[512,128]{1,0:T(8,128)S(1)}, u32[]{:S(2)}, u32[]{:S(2)}) collective-permute-start(f32[512,128]{1,0:T(8,128)S(1)} %shard_map.49.refs_3_.refs_6_), channel_id=1, source_target_pairs={{0,124},{4,8},{8,4},{12,16},{16,12},{20,24},{24,20},{28,32},{32,28... | collective-permute-start | bytes 786440 | tf_op jit(solution)/shard_map/ppermute | solution.py:245
  26.9 1.3 %shard_map.53.refs_3_.refs_6_ = f32[512,128]{1,0:T(8,128)S(1)} custom-call(f32[1]{0:T(128)S(6)} %copy.6.refs_0_, f32[64,128]{1,0:T(8,128)S(1)} %bitcast.13, bf16[192,1728]{1,0:T(8,128)(2,1)S(1)} %shard_map.46.refs_2_, f32[512,128]{1,0:T(8,128)S(1)} %shard_map.52.refs_3_.refs_6_, f32[512,128]{1,0:T(8,128)S(1)} %collective-permute-done.10.refs_4_, ...), custom_call_target="tpu_custom_call" | custom-call | tf_op jit(solution)/shard_map/pallas_call | solution.py:113
  28.2 1.5 %collective-permute-start.12 = (f32[512,128]{1,0:T(8,128)S(1)}, f32[512,128]{1,0:T(8,128)S(1)}, u32[]{:S(2)}, u32[]{:S(2)}) collective-permute-start(f32[512,128]{1,0:T(8,128)S(1)} %shard_map.53.refs_3_.refs_6_), channel_id=1, source_target_pairs={{0,124},{4,8},{8,4},{12,16},{16,12},{20,24},{24,20},{28,32},{32,28... | collective-permute-start | bytes 786440 | tf_op jit(solution)/shard_map/ppermute | solution.py:245
  29.7 1.5 %collective-permute-done.4.refs_4_ = f32[512,128]{1,0:T(8,128)S(1)} collective-permute-done((f32[512,128]{1,0:T(8,128)S(1)}, f32[512,128]{1,0:T(8,128)S(1)}, u32[]{:S(2)}, u32[]{:S(2)}) %collective-permute-start.4) | collective-permute-done | bytes 262176 | tf_op jit(solution)/shard_map/ppermute | solution.py:245
  31.3 1.3 %shard_map.50.refs_3_ = f32[512,128]{1,0:T(8,128)S(1)} custom-call(f32[1]{0:T(128)S(6)} %copy.6.refs_0_, f32[64,128]{1,0:T(8,128)S(1)} %bitcast.14, bf16[192,1728]{1,0:T(8,128)(2,1)S(1)} %shard_map.46.refs_2_, f32[512,128]{1,0:T(8,128)S(1)} %shard_map.49.refs_3_.refs_6_, f32[512,128]{1,0:T(8,128)S(1)} %collective-permute-done.4.refs_4_, ...), custom_call_target="tpu_custom_call" | custom-call | tf_op jit(solution)/shard_map/pallas_call | solution.py:113
  32.6 4.8 %collective-permute-start.6 = (f32[512,128]{1,0:T(8,128)S(1)}, f32[512,128]{1,0:T(8,128)S(1)}, u32[]{:S(2)}, u32[]{:S(2)}) collective-permute-start(f32[512,128]{1,0:T(8,128)S(1)} %shard_map.50.refs_3_), channel_id=1, source_target_pairs={{0,124},{4,8},{8,4},{12,16},{16,12},{20,24},{24,20},{28,32},{32,28... | collective-permute-start | bytes 786440 | tf_op jit(solution)/shard_map/ppermute | solution.py:245
  38.7 1.5 %collective-permute-start.14 = (f32[512,128]{1,0:T(8,128)S(1)}, f32[512,128]{1,0:T(8,128)S(1)}, u32[]{:S(2)}, u32[]{:S(2)}) collective-permute-start(f32[512,128]{1,0:T(8,128)S(1)} %shard_map.54.refs_3_), channel_id=1, source_target_pairs={{0,124},{4,8},{8,4},{12,16},{16,12},{20,24},{24,20},{28,32},{32,28... | collective-permute-start | bytes 786440 | tf_op jit(solution)/shard_map/ppermute | solution.py:245
  40.2 1.5 %collective-permute-done.6.refs_4_ = f32[512,128]{1,0:T(8,128)S(1)} collective-permute-done((f32[512,128]{1,0:T(8,128)S(1)}, f32[512,128]{1,0:T(8,128)S(1)}, u32[]{:S(2)}, u32[]{:S(2)}) %collective-permute-start.6) | collective-permute-done | bytes 262176 | tf_op jit(solution)/shard_map/ppermute | solution.py:245
  41.8 1.3 %shard_map.51.refs_0_.refs_2_ = f32[512,128]{1,0:T(8,128)S(1)} custom-call(f32[1]{0:T(128)S(6)} %copy.6.refs_0_, f32[64,128]{1,0:T(8,128)S(1)} %bitcast.16, bf16[192,1728]{1,0:T(8,128)(2,1)S(1)} %shard_map.46.refs_2_, f32[512,128]{1,0:T(8,128)S(1)} %shard_map.50.refs_3_, f32[512,128]{1,0:T(8,128)S(1)} %collective-permute-done.6.refs_4_, ...), custom_call_target="tpu_custom_call" | custom-call | tf_op jit(solution)/shard_map/pallas_call | solution.py:113
  43.1 2.1 %collective-permute-start.16 = (f32[512,128]{1,0:T(8,128)S(1)}, f32[512,128]{1,0:T(8,128)S(1)}, u32[]{:S(2)}, u32[]{:S(2)}) collective-permute-start(f32[512,128]{1,0:T(8,128)S(1)} %shard_map.51.refs_0_.refs_2_), channel_id=1, source_target_pairs={{0,1},{1,0},{2,3},{3,2},{4,7},{5,6},{6,5},{7,4},{8,9},{9,8},{10,11... | collective-permute-start | bytes 786440 | tf_op jit(solution)/shard_map/ppermute | solution.py:251
  45.2 2.7 %collective-permute-done.14.refs_4_ = f32[512,128]{1,0:T(8,128)S(1)} collective-permute-done((f32[512,128]{1,0:T(8,128)S(1)}, f32[512,128]{1,0:T(8,128)S(1)}, u32[]{:S(2)}, u32[]{:S(2)}) %collective-permute-start.14) | collective-permute-done | bytes 262176 | tf_op jit(solution)/shard_map/ppermute | solution.py:245
  49.2 2.0 %collective-permute-start.17 = (f32[512,128]{1,0:T(8,128)S(1)}, f32[512,128]{1,0:T(8,128)S(1)}, u32[]{:S(2)}, u32[]{:S(2)}) collective-permute-start(f32[512,128]{1,0:T(8,128)S(1)} %shard_map.55.refs_1_.refs_3_), channel_id=1, source_target_pairs={{0,1},{1,0},{2,3},{3,2},{4,7},{5,6},{6,5},{7,4},{8,9},{9,8},{10,11... | collective-permute-start | bytes 786440 | tf_op jit(solution)/shard_map/ppermute | solution.py:253
  51.2 2.5 %collective-permute-start.20 = (f32[512,128]{1,0:T(8,128)S(1)}, f32[512,128]{1,0:T(8,128)S(1)}, u32[]{:S(2)}, u32[]{:S(2)}) collective-permute-start(f32[512,128]{1,0:T(8,128)S(1)} %shard_map.51.refs_0_.refs_2_), channel_id=1, source_target_pairs={{0,3},{1,2},{2,1},{3,0},{4,5},{5,4},{6,7},{7,6},{8,11},{9,10},{10,... | collective-permute-start | bytes 786440 | tf_op jit(solution)/shard_map/ppermute | solution.py:252
  54.5 2.5 %collective-permute-start.18 = (f32[512,128]{1,0:T(8,128)S(1)}, f32[512,128]{1,0:T(8,128)S(1)}, u32[]{:S(2)}, u32[]{:S(2)}) collective-permute-start(f32[512,128]{1,0:T(8,128)S(1)} %collective-permute-done.16.refs_2_.refs_4_), channel_id=1, source_target_pairs={{0,3},{1,2},{2,1},{3,0},{4,5},{5,4},{6,7},{7,6},{8,11},{9,10},{10,... | collective-permute-start | bytes 786440 | tf_op jit(solution)/shard_map/ppermute | solution.py:255
  58.2 4.3 %collective-permute-start.19 = (f32[512,128]{1,0:T(8,128)S(1)}, f32[512,128]{1,0:T(8,128)S(1)}, u32[]{:S(2)}, u32[]{:S(2)}) collective-permute-start(f32[512,128]{1,0:T(8,128)S(1)} %collective-permute-done.17.refs_3_.refs_5_), channel_id=1, source_target_pairs={{0,3},{1,2},{2,1},{3,0},{4,5},{5,4},{6,7},{7,6},{8,11},{9,10},{10,... | collective-permute-start | bytes 786440 | tf_op jit(solution)/shard_map/ppermute | solution.py:256
  62.5 1.9 %collective-permute-done.18.refs_4_.refs_6_ = f32[512,128]{1,0:T(8,128)S(1)} collective-permute-done((f32[512,128]{1,0:T(8,128)S(1)}, f32[512,128]{1,0:T(8,128)S(1)}, u32[]{:S(2)}, u32[]{:S(2)}) %collective-permute-start.18) | collective-permute-done | bytes 262176 | tf_op jit(solution)/shard_map/ppermute | solution.py:255
  64.4 2.8 %collective-permute-done.19.refs_5_.refs_7_ = f32[512,128]{1,0:T(8,128)S(1)} collective-permute-done((f32[512,128]{1,0:T(8,128)S(1)}, f32[512,128]{1,0:T(8,128)S(1)}, u32[]{:S(2)}, u32[]{:S(2)}) %collective-permute-start.19) | collective-permute-done | bytes 262176 | tf_op jit(solution)/shard_map/ppermute | solution.py:256
  69.6 12.3 %all_to_all.5.refs_1_ = f32[16,24,128]{2,1,0:T(8,128)S(1)} all-to-all(f32[16,24,128]{2,1,0:T(8,128)S(1)} %broadcast_in_dim.3), channel_id=1, replica_groups=mesh['chip'=16,'core'=2,'vecs'=4] {'chip'}, dimensions={0} | all-to-all | bytes 393216 | tf_op jit(solution)/shard_map/all_to_all | solution.py:262
  82.0 1.6 %shard_map.57 = f32[1024,128]{1,0:T(8,128)} custom-call(s32[1]{0:T(128)} %bitcast.flag.refs_0_, f32[16,24,128]{2,1,0:T(8,128)S(1)} %all_to_all.5.refs_1_, f32[512,128]{1,0:T(8,128)S(1)} %shard_map.51.refs_0_.refs_2_, f32[512,128]{1,0:T(8,128)S(1)} %shard_map.55.refs_1_.refs_3_, f32[512,128]{1,0:T(8,128)S(1)} %collective-permute-done.16.refs_2_.refs_4_, ...), custom_call_target="tpu_custom_call" | custom-call | tf_op jit(solution)/shard_map/pallas_call | solution.py:216
  (44 shorter events, 14.3 us)
Async XLA Ops:
  1.1 9.2 %collective-permute-start = (f32[512,128]{1,0:T(8,128)S(1)}, f32[512,128]{1,0:T(8,128)S(1)}, u32[]{:S(2)}, u32[]{:S(2)}) collective-permute-start(f32[512,128]{1,0:T(8,128)S(1)} %bitcast.22), channel_id=1, source_target_pairs={{0,124},{4,8},{8,4},{12,16},{16,12},{20,24},{24,20},{28,32},{32,28... | collective-permute-start | bytes 786440 | tf_op jit(solution)/shard_map/ppermute | solution.py:245
  5.9 4.4 %collective-permute-start.1 = (f32[512,128]{1,0:T(8,128)S(1)}, f32[512,128]{1,0:T(8,128)S(1)}, u32[]{:S(2)}, u32[]{:S(2)}) collective-permute-start(f32[512,128]{1,0:T(8,128)S(1)} %bitcast.23), channel_id=1, source_target_pairs={{0,4},{4,0},{1,5},{5,1},{2,6},{6,2},{3,7},{7,3},{8,12},{12,8},{9,1... | collective-permute-start | bytes 786440 | tf_op jit(solution)/shard_map/ppermute | solution.py:246
  6.0 10.5 %collective-permute-start.8 = (f32[512,128]{1,0:T(8,128)S(1)}, f32[512,128]{1,0:T(8,128)S(1)}, u32[]{:S(2)}, u32[]{:S(2)}) collective-permute-start(f32[512,128]{1,0:T(8,128)S(1)} %bitcast.18), channel_id=1, source_target_pairs={{0,124},{4,8},{8,4},{12,16},{16,12},{20,24},{24,20},{28,32},{32,28... | collective-permute-start | bytes 786440 | tf_op jit(solution)/shard_map/ppermute | solution.py:245
  6.9 9.6 %collective-permute-start.9 = (f32[512,128]{1,0:T(8,128)S(1)}, f32[512,128]{1,0:T(8,128)S(1)}, u32[]{:S(2)}, u32[]{:S(2)}) collective-permute-start(f32[512,128]{1,0:T(8,128)S(1)} %bitcast.19), channel_id=1, source_target_pairs={{0,4},{4,0},{1,5},{5,1},{2,6},{6,2},{3,7},{7,3},{8,12},{12,8},{9,1... | collective-permute-start | bytes 786440 | tf_op jit(solution)/shard_map/ppermute | solution.py:246
  8.8 1.5 %copy-start = (f32[64,1,128]{2,1,0:T(1,128)S(1)}, f32[64,1,128]{2,1,0:T(1,128)}, u32[]{:S(2)}) copy-start(f32[64,1,128]{2,1,0:T(1,128)} %param.5) | copy-start | bytes 98308
  11.6 9.2 %collective-permute-start.2 = (f32[512,128]{1,0:T(8,128)S(1)}, f32[512,128]{1,0:T(8,128)S(1)}, u32[]{:S(2)}, u32[]{:S(2)}) collective-permute-start(f32[512,128]{1,0:T(8,128)S(1)} %shard_map.48.refs_3_.refs_6_), channel_id=1, source_target_pairs={{0,124},{4,8},{8,4},{12,16},{16,12},{20,24},{24,20},{28,32},{32,28... | collective-permute-start | bytes 786440 | tf_op jit(solution)/shard_map/ppermute | solution.py:245
  16.4 4.4 %collective-permute-start.3 = (f32[512,128]{1,0:T(8,128)S(1)}, f32[512,128]{1,0:T(8,128)S(1)}, u32[]{:S(2)}, u32[]{:S(2)}) collective-permute-start(f32[512,128]{1,0:T(8,128)S(1)} %shard_map.48.refs_3_.refs_6_), channel_id=1, source_target_pairs={{0,4},{4,0},{1,5},{5,1},{2,6},{6,2},{3,7},{7,3},{8,12},{12,8},{9,1... | collective-permute-start | bytes 786440 | tf_op jit(solution)/shard_map/ppermute | solution.py:246
  17.7 9.2 %collective-permute-start.10 = (f32[512,128]{1,0:T(8,128)S(1)}, f32[512,128]{1,0:T(8,128)S(1)}, u32[]{:S(2)}, u32[]{:S(2)}) collective-permute-start(f32[512,128]{1,0:T(8,128)S(1)} %shard_map.52.refs_3_.refs_6_), channel_id=1, source_target_pairs={{0,124},{4,8},{8,4},{12,16},{16,12},{20,24},{24,20},{28,32},{32,28... | collective-permute-start | bytes 786440 | tf_op jit(solution)/shard_map/ppermute | solution.py:245
  19.2 7.7 %collective-permute-start.11 = (f32[512,128]{1,0:T(8,128)S(1)}, f32[512,128]{1,0:T(8,128)S(1)}, u32[]{:S(2)}, u32[]{:S(2)}) collective-permute-start(f32[512,128]{1,0:T(8,128)S(1)} %shard_map.52.refs_3_.refs_6_), channel_id=1, source_target_pairs={{0,4},{4,0},{1,5},{5,1},{2,6},{6,2},{3,7},{7,3},{8,12},{12,8},{9,1... | collective-permute-start | bytes 786440 | tf_op jit(solution)/shard_map/ppermute | solution.py:246
  22.1 9.2 %collective-permute-start.4 = (f32[512,128]{1,0:T(8,128)S(1)}, f32[512,128]{1,0:T(8,128)S(1)}, u32[]{:S(2)}, u32[]{:S(2)}) collective-permute-start(f32[512,128]{1,0:T(8,128)S(1)} %shard_map.49.refs_3_.refs_6_), channel_id=1, source_target_pairs={{0,124},{4,8},{8,4},{12,16},{16,12},{20,24},{24,20},{28,32},{32,28... | collective-permute-start | bytes 786440 | tf_op jit(solution)/shard_map/ppermute | solution.py:245
  26.9 4.4 %collective-permute-start.5 = (f32[512,128]{1,0:T(8,128)S(1)}, f32[512,128]{1,0:T(8,128)S(1)}, u32[]{:S(2)}, u32[]{:S(2)}) collective-permute-start(f32[512,128]{1,0:T(8,128)S(1)} %shard_map.49.refs_3_.refs_6_), channel_id=1, source_target_pairs={{0,4},{4,0},{1,5},{5,1},{2,6},{6,2},{3,7},{7,3},{8,12},{12,8},{9,1... | collective-permute-start | bytes 786440 | tf_op jit(solution)/shard_map/ppermute | solution.py:246
  28.2 9.2 %collective-permute-start.12 = (f32[512,128]{1,0:T(8,128)S(1)}, f32[512,128]{1,0:T(8,128)S(1)}, u32[]{:S(2)}, u32[]{:S(2)}) collective-permute-start(f32[512,128]{1,0:T(8,128)S(1)} %shard_map.53.refs_3_.refs_6_), channel_id=1, source_target_pairs={{0,124},{4,8},{8,4},{12,16},{16,12},{20,24},{24,20},{28,32},{32,28... | collective-permute-start | bytes 786440 | tf_op jit(solution)/shard_map/ppermute | solution.py:245
  29.7 7.7 %collective-permute-start.13 = (f32[512,128]{1,0:T(8,128)S(1)}, f32[512,128]{1,0:T(8,128)S(1)}, u32[]{:S(2)}, u32[]{:S(2)}) collective-permute-start(f32[512,128]{1,0:T(8,128)S(1)} %shard_map.53.refs_3_.refs_6_), channel_id=1, source_target_pairs={{0,4},{4,0},{1,5},{5,1},{2,6},{6,2},{3,7},{7,3},{8,12},{12,8},{9,1... | collective-permute-start | bytes 786440 | tf_op jit(solution)/shard_map/ppermute | solution.py:246
  32.6 9.2 %collective-permute-start.6 = (f32[512,128]{1,0:T(8,128)S(1)}, f32[512,128]{1,0:T(8,128)S(1)}, u32[]{:S(2)}, u32[]{:S(2)}) collective-permute-start(f32[512,128]{1,0:T(8,128)S(1)} %shard_map.50.refs_3_), channel_id=1, source_target_pairs={{0,124},{4,8},{8,4},{12,16},{16,12},{20,24},{24,20},{28,32},{32,28... | collective-permute-start | bytes 786440 | tf_op jit(solution)/shard_map/ppermute | solution.py:245
  37.4 4.4 %collective-permute-start.7 = (f32[512,128]{1,0:T(8,128)S(1)}, f32[512,128]{1,0:T(8,128)S(1)}, u32[]{:S(2)}, u32[]{:S(2)}) collective-permute-start(f32[512,128]{1,0:T(8,128)S(1)} %shard_map.50.refs_3_), channel_id=1, source_target_pairs={{0,4},{4,0},{1,5},{5,1},{2,6},{6,2},{3,7},{7,3},{8,12},{12,8},{9,1... | collective-permute-start | bytes 786440 | tf_op jit(solution)/shard_map/ppermute | solution.py:246
  38.7 9.2 %collective-permute-start.14 = (f32[512,128]{1,0:T(8,128)S(1)}, f32[512,128]{1,0:T(8,128)S(1)}, u32[]{:S(2)}, u32[]{:S(2)}) collective-permute-start(f32[512,128]{1,0:T(8,128)S(1)} %shard_map.54.refs_3_), channel_id=1, source_target_pairs={{0,124},{4,8},{8,4},{12,16},{16,12},{20,24},{24,20},{28,32},{32,28... | collective-permute-start | bytes 786440 | tf_op jit(solution)/shard_map/ppermute | solution.py:245
  40.2 7.7 %collective-permute-start.15 = (f32[512,128]{1,0:T(8,128)S(1)}, f32[512,128]{1,0:T(8,128)S(1)}, u32[]{:S(2)}, u32[]{:S(2)}) collective-permute-start(f32[512,128]{1,0:T(8,128)S(1)} %shard_map.54.refs_3_), channel_id=1, source_target_pairs={{0,4},{4,0},{1,5},{5,1},{2,6},{6,2},{3,7},{7,3},{8,12},{12,8},{9,1... | collective-permute-start | bytes 786440 | tf_op jit(solution)/shard_map/ppermute | solution.py:246
  43.1 11.4 %collective-permute-start.16 = (f32[512,128]{1,0:T(8,128)S(1)}, f32[512,128]{1,0:T(8,128)S(1)}, u32[]{:S(2)}, u32[]{:S(2)}) collective-permute-start(f32[512,128]{1,0:T(8,128)S(1)} %shard_map.51.refs_0_.refs_2_), channel_id=1, source_target_pairs={{0,1},{1,0},{2,3},{3,2},{4,7},{5,6},{6,5},{7,4},{8,9},{9,8},{10,11... | collective-permute-start | bytes 786440 | tf_op jit(solution)/shard_map/ppermute | solution.py:251
  49.2 9.0 %collective-permute-start.17 = (f32[512,128]{1,0:T(8,128)S(1)}, f32[512,128]{1,0:T(8,128)S(1)}, u32[]{:S(2)}, u32[]{:S(2)}) collective-permute-start(f32[512,128]{1,0:T(8,128)S(1)} %shard_map.55.refs_1_.refs_3_), channel_id=1, source_target_pairs={{0,1},{1,0},{2,3},{3,2},{4,7},{5,6},{6,5},{7,4},{8,9},{9,8},{10,11... | collective-permute-start | bytes 786440 | tf_op jit(solution)/shard_map/ppermute | solution.py:253
  51.2 11.3 %collective-permute-start.20 = (f32[512,128]{1,0:T(8,128)S(1)}, f32[512,128]{1,0:T(8,128)S(1)}, u32[]{:S(2)}, u32[]{:S(2)}) collective-permute-start(f32[512,128]{1,0:T(8,128)S(1)} %shard_map.51.refs_0_.refs_2_), channel_id=1, source_target_pairs={{0,3},{1,2},{2,1},{3,0},{4,5},{5,4},{6,7},{7,6},{8,11},{9,10},{10,... | collective-permute-start | bytes 786440 | tf_op jit(solution)/shard_map/ppermute | solution.py:252
  53.8 8.8 %collective-permute-start.21 = (f32[512,128]{1,0:T(8,128)S(1)}, f32[512,128]{1,0:T(8,128)S(1)}, u32[]{:S(2)}, u32[]{:S(2)}) collective-permute-start(f32[512,128]{1,0:T(8,128)S(1)} %shard_map.55.refs_1_.refs_3_), channel_id=1, source_target_pairs={{0,3},{1,2},{2,1},{3,0},{4,5},{5,4},{6,7},{7,6},{8,11},{9,10},{10,... | collective-permute-start | bytes 786440 | tf_op jit(solution)/shard_map/ppermute | solution.py:254
  54.5 10.0 %collective-permute-start.18 = (f32[512,128]{1,0:T(8,128)S(1)}, f32[512,128]{1,0:T(8,128)S(1)}, u32[]{:S(2)}, u32[]{:S(2)}) collective-permute-start(f32[512,128]{1,0:T(8,128)S(1)} %collective-permute-done.16.refs_2_.refs_4_), channel_id=1, source_target_pairs={{0,3},{1,2},{2,1},{3,0},{4,5},{5,4},{6,7},{7,6},{8,11},{9,10},{10,... | collective-permute-start | bytes 786440 | tf_op jit(solution)/shard_map/ppermute | solution.py:255
  58.2 9.0 %collective-permute-start.19 = (f32[512,128]{1,0:T(8,128)S(1)}, f32[512,128]{1,0:T(8,128)S(1)}, u32[]{:S(2)}, u32[]{:S(2)}) collective-permute-start(f32[512,128]{1,0:T(8,128)S(1)} %collective-permute-done.17.refs_3_.refs_5_), channel_id=1, source_target_pairs={{0,3},{1,2},{2,1},{3,0},{4,5},{5,4},{6,7},{7,6},{8,11},{9,10},{10,... | collective-permute-start | bytes 786440 | tf_op jit(solution)/shard_map/ppermute | solution.py:256
  68.4 1.2 %collective-permute-start.22 = (f32[24,128]{1,0:T(8,128)S(1)}, f32[24,128]{1,0:T(8,128)S(1)}, u32[]{:S(2)}, u32[]{:S(2)}) collective-permute-start(f32[24,128]{1,0:T(8,128)S(1)} %shard_map.56), channel_id=1, source_target_pairs={{0,4},{4,0},{1,5},{5,1},{2,6},{6,2},{3,7},{7,3},{8,12},{12,8},{9,1... | collective-permute-start | bytes 36872 | tf_op jit(solution)/shard_map/ppermute | solution.py:260
  (2 other events, 2.2 us)
where the time goes:
time: 83.8 us; the launch traced here: 83.5 us
  starting transfers between devices  39.1 us (47%)
  waiting for transfers between devices  14.8 us (18%)
  Pallas kernels  14.3 us (17%)
  blocking collectives  12.3 us (15%)
  local copies, waits for them, and re-layouts  2.23 us (3%)
    ppermute x8, starting transfers between devices, filtered(): away = lax.ppermute(cur[h], cells, outer)  24.8 us
    all_to_all x1, blocking collectives, filtered(): lax.all_to_all(jnp.broadcast_to(gram, (chips, *gram.shape)), 'chip', spli...  12.3 us
    pallas_call x8, Pallas kernels, apply_step(): pl.pallas_call(lambda *refs: step_body(first, *refs), in_specs=[pl.BlockS...  10.3 us
    ppermute x8, waiting for transfers between devices, filtered(): away = lax.ppermute(cur[h], cells, outer)  7.67 us
    ppermute x1, starting transfers between devices, filtered(): b_far = lax.ppermute(b_early, planes, late)  4.32 us
    ppermute x1, waiting for transfers between devices, filtered(): b_far = lax.ppermute(b_early, planes, late)  2.81 us
    ppermute x1, starting transfers between devices, filtered(): a_far = lax.ppermute(a_early, planes, late)  2.53 us
    ppermute x1, starting transfers between devices, filtered(): a_late = lax.ppermute(a, planes, late)  2.53 us
  transfers between devices with their start and end apart: 23, of which 9 were waited for; matrix products, arithmetic and copies ran while one was open for 0% of the time, Pallas kernels for 14%

commit v1 on v0

--- a/solution.py
+++ b/solution.py
@@ -79,31 +79,27 @@
         center, pot, w, cur, left, right, prev, out = refs
     onsite = pot[...] - center[0]
     lane = lax.broadcasted_iota(jnp.int32, (ORB, CELLS), 1) % NZ
-    for pair in range(HALF // 2):
-        rows = [pl.ds(2 * pair + i, ORB, stride=HALF) for i in range(2)]
-        own = [cur[r, :] for r in rows]
-        columns = []
-        for i in range(2):
-            here = jnp.concatenate([left[rows[i], :], own[i], right[rows[i], :]], axis=0)
-            below, above = pltpu.roll(here, NZ, 1), pltpu.roll(here, CELLS - NZ, 1)
-            columns.append(jnp.concatenate([below, here, above], axis=0))
-        high, low = split(jnp.concatenate(columns, axis=1))
-        stacked = jnp.concatenate([high, low, high], axis=0)
-        product = jnp.dot(w[...], stacked, preferred_element_type=F32)
-        for i in range(2):
-            below, here, above = (
-                product[iz * ORB : (iz + 1) * ORB, i * CELLS : (i + 1) * CELLS] for iz in range(3)
-            )
-            below = jnp.where(
-                lane == 0, pltpu.roll(below, CELLS - NZ + 1, 1), pltpu.roll(below, 1, 1)
-            )
-            above = jnp.where(
-                lane == NZ - 1, pltpu.roll(above, NZ - 1, 1), pltpu.roll(above, CELLS - 1, 1)
-            )
-            total = onsite * own[i] + here + below + above
-            if not first:
-                total = 2.0 * total - prev[rows[i], :]
-            out[rows[i], :] = total
+    rows = [pl.ds(i, ORB, stride=HALF) for i in range(HALF)]
+    columns = []
+    for r in rows:
+        here = jnp.concatenate([left[r, :], cur[r, :], right[r, :]], axis=0)
+        below, above = pltpu.roll(here, NZ, 1), pltpu.roll(here, CELLS - NZ, 1)
+        columns.append(jnp.concatenate([below, here, above], axis=0))
+    high, low = split(jnp.concatenate(columns, axis=1))
+    stacked = jnp.concatenate([high, low, high], axis=0)
+    product = jnp.dot(w[...], stacked, preferred_element_type=F32)
+    for i, r in enumerate(rows):
+        below, here, above = (
+            product[iz * ORB : (iz + 1) * ORB, i * CELLS : (i + 1) * CELLS] for iz in range(3)
+        )
+        below = jnp.where(lane == 0, pltpu.roll(below, CELLS - NZ + 1, 1), pltpu.roll(below, 1, 1))
+        above = jnp.where(
+            lane == NZ - 1, pltpu.roll(above, NZ - 1, 1), pltpu.roll(above, CELLS - 1, 1)
+        )
+        total = onsite * cur[r, :] + here + below + above
+        if not first:
+            total = 2.0 * total - prev[r, :]
+        out[r, :] = total
 
 
 def apply_step(center, pot, w, cur, left, right, prev=None):
@@ -126,7 +122,7 @@
 
 def gram_body(flag, *refs):
     pieces, out = refs[:-1], refs[-1]
-    total = jnp.zeros((NVEC, 2 * NVEC), F32)
+    total = jnp.zeros((2 * NVEC, NVEC), F32)
     for o in range(0, ORB, 2):
         rows = jnp.concatenate(
             [
@@ -138,10 +134,10 @@
         high, low = split(rows)
         both = jnp.concatenate([high, low], axis=0)
         total = total + lax.dot_general(
-            high, both, (((1,), (1,)), ((), ())), preferred_element_type=F32
-        )
-    cross = total[:, NVEC:]
-    gram = total[:, :NVEC] + cross + jnp.transpose(cross)
+            both, high, (((1,), (1,)), ((), ())), preferred_element_type=F32
+        )
+    cross = total[NVEC:]
+    gram = total[:NVEC] + cross + jnp.transpose(cross)
     gram = changed_over(changed_over(gram, flag, 0), flag, 1)
     q = NVEC // 4
     out[: q, :] = jnp.concatenate(
@@ -163,7 +159,8 @@
 
 
 def mix_body(factor, flag, copies, *refs):
-    pieces, out = refs[:-1], refs[-1]
+    pieces, result, out, semaphores = refs[:-3], refs[-3], refs[-2], refs[-1]
+    transfers = []
     packed = jnp.sum(copies[...], axis=0)
     q = NVEC // 4
     row = lax.broadcasted_iota(jnp.int32, packed.shape, 0)
@@ -209,6 +206,13 @@
         for side in range(2):
             at = (group * 8 + side * 4) * 2 * HALF
             out[at : at + 8 * HALF, :] = mixed[:, side * CELLS : (side + 1) * CELLS]
+        done = pl.ds(group * 16 * HALF, 16 * HALF)
+        transfers.append(
+            pltpu.make_async_copy(out.at[done], result.at[done], semaphores.at[group])
+        )
+        transfers[-1].start()
+    for transfer in transfers:
+        transfer.wait()
 
 
 def mix(factor, flag, copies, pieces):
@@ -216,7 +220,12 @@
     return pl.pallas_call(
         lambda *refs: mix_body(factor, *refs),
         in_specs=[pl.BlockSpec(memory_space=pltpu.SMEM)] + [vmem] * (1 + len(pieces)),
+        out_specs=pl.BlockSpec(memory_space=pltpu.HBM),
         out_shape=jax.ShapeDtypeStruct((ORB * 2 * HALF, CELLS), F32),
+        scratch_shapes=[
+            pltpu.VMEM((ORB * 2 * HALF, CELLS), F32),
+            pltpu.SemaphoreType.DMA((ORB // 8,)),
+        ],
         compiler_params=LIMIT,
     )(flag, copies, *pieces)
 

time: 83.8 us -> 83.7 us (level)
  no operation moved by 1% of the time
where the time goes in v1:
time: 83.7 us; the launch traced here: 83.4 us
  starting transfers between devices  39 us (47%)
  waiting for transfers between devices  14.8 us (18%)
  Pallas kernels  14 us (17%)
  blocking collectives  12.3 us (15%)
  local copies, waits for them, and re-layouts  2.23 us (3%)
  between operations  0.91 us (1%)
    ppermute x8, starting transfers between devices, filtered(): away = lax.ppermute(cur[h], cells, outer)  24.8 us
    all_to_all x1, blocking collectives, filtered(): lax.all_to_all(jnp.broadcast_to(gram, (chips, *gram.shape)), 'chip', spli...  12.3 us
    pallas_call x8, Pallas kernels, apply_step(): pl.pallas_call(lambda *refs: step_body(first, *refs), in_specs=[pl.BlockS...  10.3 us
    ppermute x8, waiting for transfers between devices, filtered(): away = lax.ppermute(cur[h], cells, outer)  7.67 us
    ppermute x1, starting transfers between devices, filtered(): b_far = lax.ppermute(b_early, planes, late)  4.31 us
    ppermute x1, waiting for transfers between devices, filtered(): b_far = lax.ppermute(b_early, planes, late)  2.81 us
    ppermute x1, starting transfers between devices, filtered(): a_far = lax.ppermute(a_early, planes, late)  2.53 us
    ppermute x1, starting transfers between devices, filtered(): a_late = lax.ppermute(a, planes, late)  2.53 us
  transfers between devices with their start and end apart: 23, of which 9 were waited for; matrix products, arithmetic and copies ran while one was open for 0% of the time, Pallas kernels for 14%

profile of v1, /device:TPU:0, one launch (start us, length us, event | category | flops | bytes accessed | tf_op | source)
XLA Modules:
  0.0 83.4 jit_solution(7146643348257297732)
XLA Ops:
  1.1 4.8 %collective-permute-start = (f32[512,128]{1,0:T(8,128)S(1)}, f32[512,128]{1,0:T(8,128)S(1)}, u32[]{:S(2)}, u32[]{:S(2)}) collective-permute-start(f32[512,128]{1,0:T(8,128)S(1)} %bitcast.22), channel_id=1, source_target_pairs={{0,124},{4,8},{8,4},{12,16},{16,12},{20,24},{24,20},{28,32},{32,28... | collective-permute-start | bytes 786440 | tf_op jit(solution)/shard_map/ppermute | solution.py:254
  11.6 4.8 %collective-permute-start.2 = (f32[512,128]{1,0:T(8,128)S(1)}, f32[512,128]{1,0:T(8,128)S(1)}, u32[]{:S(2)}, u32[]{:S(2)}) collective-permute-start(f32[512,128]{1,0:T(8,128)S(1)} %shard_map.48.refs_3_.refs_6_), channel_id=1, source_target_pairs={{0,124},{4,8},{8,4},{12,16},{16,12},{20,24},{24,20},{28,32},{32,28... | collective-permute-start | bytes 786440 | tf_op jit(solution)/shard_map/ppermute | solution.py:254
  17.7 1.5 %collective-permute-start.10 = (f32[512,128]{1,0:T(8,128)S(1)}, f32[512,128]{1,0:T(8,128)S(1)}, u32[]{:S(2)}, u32[]{:S(2)}) collective-permute-start(f32[512,128]{1,0:T(8,128)S(1)} %shard_map.52.refs_3_.refs_6_), channel_id=1, source_target_pairs={{0,124},{4,8},{8,4},{12,16},{16,12},{20,24},{24,20},{28,32},{32,28... | collective-permute-start | bytes 786440 | tf_op jit(solution)/shard_map/ppermute | solution.py:254
  19.3 1.5 %collective-permute-done.2.refs_4_ = f32[512,128]{1,0:T(8,128)S(1)} collective-permute-done((f32[512,128]{1,0:T(8,128)S(1)}, f32[512,128]{1,0:T(8,128)S(1)}, u32[]{:S(2)}, u32[]{:S(2)}) %collective-permute-start.2) | collective-permute-done | bytes 262176 | tf_op jit(solution)/shard_map/ppermute | solution.py:254
  20.8 1.3 %shard_map.49.refs_3_.refs_6_ = f32[512,128]{1,0:T(8,128)S(1)} custom-call(f32[1]{0:T(128)S(6)} %copy.6.refs_0_, f32[64,128]{1,0:T(8,128)S(1)} %bitcast.12, bf16[192,1728]{1,0:T(8,128)(2,1)S(1)} %shard_map.46.refs_2_, f32[512,128]{1,0:T(8,128)S(1)} %shard_map.48.refs_3_.refs_6_, f32[512,128]{1,0:T(8,128)S(1)} %collective-permute-done.2.refs_4_, ...), custom_call_target="tpu_custom_call" | custom-call | tf_op jit(solution)/shard_map/pallas_call | solution.py:109
  22.1 4.8 %collective-permute-start.4 = (f32[512,128]{1,0:T(8,128)S(1)}, f32[512,128]{1,0:T(8,128)S(1)}, u32[]{:S(2)}, u32[]{:S(2)}) collective-permute-start(f32[512,128]{1,0:T(8,128)S(1)} %shard_map.49.refs_3_.refs_6_), channel_id=1, source_target_pairs={{0,124},{4,8},{8,4},{12,16},{16,12},{20,24},{24,20},{28,32},{32,28... | collective-permute-start | bytes 786440 | tf_op jit(solution)/shard_map/ppermute | solution.py:254
  26.9 1.3 %shard_map.53.refs_3_.refs_6_ = f32[512,128]{1,0:T(8,128)S(1)} custom-call(f32[1]{0:T(128)S(6)} %copy.6.refs_0_, f32[64,128]{1,0:T(8,128)S(1)} %bitcast.13, bf16[192,1728]{1,0:T(8,128)(2,1)S(1)} %shard_map.46.refs_2_, f32[512,128]{1,0:T(8,128)S(1)} %shard_map.52.refs_3_.refs_6_, f32[512,128]{1,0:T(8,128)S(1)} %collective-permute-done.10.refs_4_, ...), custom_call_target="tpu_custom_call" | custom-call | tf_op jit(solution)/shard_map/pallas_call | solution.py:109
  28.2 1.5 %collective-permute-start.12 = (f32[512,128]{1,0:T(8,128)S(1)}, f32[512,128]{1,0:T(8,128)S(1)}, u32[]{:S(2)}, u32[]{:S(2)}) collective-permute-start(f32[512,128]{1,0:T(8,128)S(1)} %shard_map.53.refs_3_.refs_6_), channel_id=1, source_target_pairs={{0,124},{4,8},{8,4},{12,16},{16,12},{20,24},{24,20},{28,32},{32,28... | collective-permute-start | bytes 786440 | tf_op jit(solution)/shard_map/ppermute | solution.py:254
  29.8 1.5 %collective-permute-done.4.refs_4_ = f32[512,128]{1,0:T(8,128)S(1)} collective-permute-done((f32[512,128]{1,0:T(8,128)S(1)}, f32[512,128]{1,0:T(8,128)S(1)}, u32[]{:S(2)}, u32[]{:S(2)}) %collective-permute-start.4) | collective-permute-done | bytes 262176 | tf_op jit(solution)/shard_map/ppermute | solution.py:254
  31.3 1.3 %shard_map.50.refs_3_ = f32[512,128]{1,0:T(8,128)S(1)} custom-call(f32[1]{0:T(128)S(6)} %copy.6.refs_0_, f32[64,128]{1,0:T(8,128)S(1)} %bitcast.14, bf16[192,1728]{1,0:T(8,128)(2,1)S(1)} %shard_map.46.refs_2_, f32[512,128]{1,0:T(8,128)S(1)} %shard_map.49.refs_3_.refs_6_, f32[512,128]{1,0:T(8,128)S(1)} %collective-permute-done.4.refs_4_, ...), custom_call_target="tpu_custom_call" | custom-call | tf_op jit(solution)/shard_map/pallas_call | solution.py:109
  32.6 4.8 %collective-permute-start.6 = (f32[512,128]{1,0:T(8,128)S(1)}, f32[512,128]{1,0:T(8,128)S(1)}, u32[]{:S(2)}, u32[]{:S(2)}) collective-permute-start(f32[512,128]{1,0:T(8,128)S(1)} %shard_map.50.refs_3_), channel_id=1, source_target_pairs={{0,124},{4,8},{8,4},{12,16},{16,12},{20,24},{24,20},{28,32},{32,28... | collective-permute-start | bytes 786440 | tf_op jit(solution)/shard_map/ppermute | solution.py:254
  37.5 1.3 %shard_map.54.refs_3_ = f32[512,128]{1,0:T(8,128)S(1)} custom-call(f32[1]{0:T(128)S(6)} %copy.6.refs_0_, f32[64,128]{1,0:T(8,128)S(1)} %bitcast.15, bf16[192,1728]{1,0:T(8,128)(2,1)S(1)} %shard_map.46.refs_2_, f32[512,128]{1,0:T(8,128)S(1)} %shard_map.53.refs_3_.refs_6_, f32[512,128]{1,0:T(8,128)S(1)} %collective-permute-done.12.refs_4_, ...), custom_call_target="tpu_custom_call" | custom-call | tf_op jit(solution)/shard_map/pallas_call | solution.py:109
  38.7 1.5 %collective-permute-start.14 = (f32[512,128]{1,0:T(8,128)S(1)}, f32[512,128]{1,0:T(8,128)S(1)}, u32[]{:S(2)}, u32[]{:S(2)}) collective-permute-start(f32[512,128]{1,0:T(8,128)S(1)} %shard_map.54.refs_3_), channel_id=1, source_target_pairs={{0,124},{4,8},{8,4},{12,16},{16,12},{20,24},{24,20},{28,32},{32,28... | collective-permute-start | bytes 786440 | tf_op jit(solution)/shard_map/ppermute | solution.py:254
  40.3 1.5 %collective-permute-done.6.refs_4_ = f32[512,128]{1,0:T(8,128)S(1)} collective-permute-done((f32[512,128]{1,0:T(8,128)S(1)}, f32[512,128]{1,0:T(8,128)S(1)}, u32[]{:S(2)}, u32[]{:S(2)}) %collective-permute-start.6) | collective-permute-done | bytes 262176 | tf_op jit(solution)/shard_map/ppermute | solution.py:254
  43.1 2.1 %collective-permute-start.16 = (f32[512,128]{1,0:T(8,128)S(1)}, f32[512,128]{1,0:T(8,128)S(1)}, u32[]{:S(2)}, u32[]{:S(2)}) collective-permute-start(f32[512,128]{1,0:T(8,128)S(1)} %shard_map.51.refs_0_.refs_2_), channel_id=1, source_target_pairs={{0,1},{1,0},{2,3},{3,2},{4,7},{5,6},{6,5},{7,4},{8,9},{9,8},{10,11... | collective-permute-start | bytes 786440 | tf_op jit(solution)/shard_map/ppermute | solution.py:260
  45.2 2.7 %collective-permute-done.14.refs_4_ = f32[512,128]{1,0:T(8,128)S(1)} collective-permute-done((f32[512,128]{1,0:T(8,128)S(1)}, f32[512,128]{1,0:T(8,128)S(1)}, u32[]{:S(2)}, u32[]{:S(2)}) %collective-permute-start.14) | collective-permute-done | bytes 262176 | tf_op jit(solution)/shard_map/ppermute | solution.py:254
  49.2 2.0 %collective-permute-start.17 = (f32[512,128]{1,0:T(8,128)S(1)}, f32[512,128]{1,0:T(8,128)S(1)}, u32[]{:S(2)}, u32[]{:S(2)}) collective-permute-start(f32[512,128]{1,0:T(8,128)S(1)} %shard_map.55.refs_1_.refs_3_), channel_id=1, source_target_pairs={{0,1},{1,0},{2,3},{3,2},{4,7},{5,6},{6,5},{7,4},{8,9},{9,8},{10,11... | collective-permute-start | bytes 786440 | tf_op jit(solution)/shard_map/ppermute | solution.py:262
  51.2 2.5 %collective-permute-start.20 = (f32[512,128]{1,0:T(8,128)S(1)}, f32[512,128]{1,0:T(8,128)S(1)}, u32[]{:S(2)}, u32[]{:S(2)}) collective-permute-start(f32[512,128]{1,0:T(8,128)S(1)} %shard_map.51.refs_0_.refs_2_), channel_id=1, source_target_pairs={{0,3},{1,2},{2,1},{3,0},{4,5},{5,4},{6,7},{7,6},{8,11},{9,10},{10,... | collective-permute-start | bytes 786440 | tf_op jit(solution)/shard_map/ppermute | solution.py:261
  54.5 2.5 %collective-permute-start.18 = (f32[512,128]{1,0:T(8,128)S(1)}, f32[512,128]{1,0:T(8,128)S(1)}, u32[]{:S(2)}, u32[]{:S(2)}) collective-permute-start(f32[512,128]{1,0:T(8,128)S(1)} %collective-permute-done.16.refs_2_.refs_4_), channel_id=1, source_target_pairs={{0,3},{1,2},{2,1},{3,0},{4,5},{5,4},{6,7},{7,6},{8,11},{9,10},{10,... | collective-permute-start | bytes 786440 | tf_op jit(solution)/shard_map/ppermute | solution.py:264
  58.2 4.3 %collective-permute-start.19 = (f32[512,128]{1,0:T(8,128)S(1)}, f32[512,128]{1,0:T(8,128)S(1)}, u32[]{:S(2)}, u32[]{:S(2)}) collective-permute-start(f32[512,128]{1,0:T(8,128)S(1)} %collective-permute-done.17.refs_3_.refs_5_), channel_id=1, source_target_pairs={{0,3},{1,2},{2,1},{3,0},{4,5},{5,4},{6,7},{7,6},{8,11},{9,10},{10,... | collective-permute-start | bytes 786440 | tf_op jit(solution)/shard_map/ppermute | solution.py:265
  62.6 1.9 %collective-permute-done.18.refs_4_.refs_6_ = f32[512,128]{1,0:T(8,128)S(1)} collective-permute-done((f32[512,128]{1,0:T(8,128)S(1)}, f32[512,128]{1,0:T(8,128)S(1)}, u32[]{:S(2)}, u32[]{:S(2)}) %collective-permute-start.18) | collective-permute-done | bytes 262176 | tf_op jit(solution)/shard_map/ppermute | solution.py:264
  64.4 2.8 %collective-permute-done.19.refs_5_.refs_7_ = f32[512,128]{1,0:T(8,128)S(1)} collective-permute-done((f32[512,128]{1,0:T(8,128)S(1)}, f32[512,128]{1,0:T(8,128)S(1)}, u32[]{:S(2)}, u32[]{:S(2)}) %collective-permute-start.19) | collective-permute-done | bytes 262176 | tf_op jit(solution)/shard_map/ppermute | solution.py:265
  69.4 12.3 %all_to_all.5.refs_1_ = f32[16,24,128]{2,1,0:T(8,128)S(1)} all-to-all(f32[16,24,128]{2,1,0:T(8,128)S(1)} %broadcast_in_dim.3), channel_id=1, replica_groups=mesh['chip'=16,'core'=2,'vecs'=4] {'chip'}, dimensions={0} | all-to-all | bytes 393216 | tf_op jit(solution)/shard_map/all_to_all | solution.py:271
  81.8 1.5 %shard_map.57 = f32[1024,128]{1,0:T(8,128)} custom-call(s32[1]{0:T(128)} %bitcast.flag.refs_0_, f32[16,24,128]{2,1,0:T(8,128)S(1)} %all_to_all.5.refs_1_, f32[512,128]{1,0:T(8,128)S(1)} %shard_map.51.refs_0_.refs_2_, f32[512,128]{1,0:T(8,128)S(1)} %shard_map.55.refs_1_.refs_3_, f32[512,128]{1,0:T(8,128)S(1)} %collective-permute-done.16.refs_2_.refs_4_, ...), custom_call_target="tpu_custom_call" | custom-call | tf_op jit(solution)/shard_map/pallas_call | solution.py:220
  (44 shorter events, 14.1 us)
Async XLA Ops:
  1.1 9.2 %collective-permute-start = (f32[512,128]{1,0:T(8,128)S(1)}, f32[512,128]{1,0:T(8,128)S(1)}, u32[]{:S(2)}, u32[]{:S(2)}) collective-permute-start(f32[512,128]{1,0:T(8,128)S(1)} %bitcast.22), channel_id=1, source_target_pairs={{0,124},{4,8},{8,4},{12,16},{16,12},{20,24},{24,20},{28,32},{32,28... | collective-permute-start | bytes 786440 | tf_op jit(solution)/shard_map/ppermute | solution.py:254
  5.9 4.4 %collective-permute-start.1 = (f32[512,128]{1,0:T(8,128)S(1)}, f32[512,128]{1,0:T(8,128)S(1)}, u32[]{:S(2)}, u32[]{:S(2)}) collective-permute-start(f32[512,128]{1,0:T(8,128)S(1)} %bitcast.23), channel_id=1, source_target_pairs={{0,4},{4,0},{1,5},{5,1},{2,6},{6,2},{3,7},{7,3},{8,12},{12,8},{9,1... | collective-permute-start | bytes 786440 | tf_op jit(solution)/shard_map/ppermute | solution.py:255
  6.0 10.5 %collective-permute-start.8 = (f32[512,128]{1,0:T(8,128)S(1)}, f32[512,128]{1,0:T(8,128)S(1)}, u32[]{:S(2)}, u32[]{:S(2)}) collective-permute-start(f32[512,128]{1,0:T(8,128)S(1)} %bitcast.18), channel_id=1, source_target_pairs={{0,124},{4,8},{8,4},{12,16},{16,12},{20,24},{24,20},{28,32},{32,28... | collective-permute-start | bytes 786440 | tf_op jit(solution)/shard_map/ppermute | solution.py:254
  6.9 9.6 %collective-permute-start.9 = (f32[512,128]{1,0:T(8,128)S(1)}, f32[512,128]{1,0:T(8,128)S(1)}, u32[]{:S(2)}, u32[]{:S(2)}) collective-permute-start(f32[512,128]{1,0:T(8,128)S(1)} %bitcast.19), channel_id=1, source_target_pairs={{0,4},{4,0},{1,5},{5,1},{2,6},{6,2},{3,7},{7,3},{8,12},{12,8},{9,1... | collective-permute-start | bytes 786440 | tf_op jit(solution)/shard_map/ppermute | solution.py:255
  8.8 1.5 %copy-start = (f32[64,1,128]{2,1,0:T(1,128)S(1)}, f32[64,1,128]{2,1,0:T(1,128)}, u32[]{:S(2)}) copy-start(f32[64,1,128]{2,1,0:T(1,128)} %param.5) | copy-start | bytes 98308
  11.6 9.2 %collective-permute-start.2 = (f32[512,128]{1,0:T(8,128)S(1)}, f32[512,128]{1,0:T(8,128)S(1)}, u32[]{:S(2)}, u32[]{:S(2)}) collective-permute-start(f32[512,128]{1,0:T(8,128)S(1)} %shard_map.48.refs_3_.refs_6_), channel_id=1, source_target_pairs={{0,124},{4,8},{8,4},{12,16},{16,12},{20,24},{24,20},{28,32},{32,28... | collective-permute-start | bytes 786440 | tf_op jit(solution)/shard_map/ppermute | solution.py:254
  16.4 4.4 %collective-permute-start.3 = (f32[512,128]{1,0:T(8,128)S(1)}, f32[512,128]{1,0:T(8,128)S(1)}, u32[]{:S(2)}, u32[]{:S(2)}) collective-permute-start(f32[512,128]{1,0:T(8,128)S(1)} %shard_map.48.refs_3_.refs_6_), channel_id=1, source_target_pairs={{0,4},{4,0},{1,5},{5,1},{2,6},{6,2},{3,7},{7,3},{8,12},{12,8},{9,1... | collective-permute-start | bytes 786440 | tf_op jit(solution)/shard_map/ppermute | solution.py:255
  17.7 9.2 %collective-permute-start.10 = (f32[512,128]{1,0:T(8,128)S(1)}, f32[512,128]{1,0:T(8,128)S(1)}, u32[]{:S(2)}, u32[]{:S(2)}) collective-permute-start(f32[512,128]{1,0:T(8,128)S(1)} %shard_map.52.refs_3_.refs_6_), channel_id=1, source_target_pairs={{0,124},{4,8},{8,4},{12,16},{16,12},{20,24},{24,20},{28,32},{32,28... | collective-permute-start | bytes 786440 | tf_op jit(solution)/shard_map/ppermute | solution.py:254
  19.2 7.7 %collective-permute-start.11 = (f32[512,128]{1,0:T(8,128)S(1)}, f32[512,128]{1,0:T(8,128)S(1)}, u32[]{:S(2)}, u32[]{:S(2)}) collective-permute-start(f32[512,128]{1,0:T(8,128)S(1)} %shard_map.52.refs_3_.refs_6_), channel_id=1, source_target_pairs={{0,4},{4,0},{1,5},{5,1},{2,6},{6,2},{3,7},{7,3},{8,12},{12,8},{9,1... | collective-permute-start | bytes 786440 | tf_op jit(solution)/shard_map/ppermute | solution.py:255
  22.1 9.2 %collective-permute-start.4 = (f32[512,128]{1,0:T(8,128)S(1)}, f32[512,128]{1,0:T(8,128)S(1)}, u32[]{:S(2)}, u32[]{:S(2)}) collective-permute-start(f32[512,128]{1,0:T(8,128)S(1)} %shard_map.49.refs_3_.refs_6_), channel_id=1, source_target_pairs={{0,124},{4,8},{8,4},{12,16},{16,12},{20,24},{24,20},{28,32},{32,28... | collective-permute-start | bytes 786440 | tf_op jit(solution)/shard_map/ppermute | solution.py:254
  26.9 4.4 %collective-permute-start.5 = (f32[512,128]{1,0:T(8,128)S(1)}, f32[512,128]{1,0:T(8,128)S(1)}, u32[]{:S(2)}, u32[]{:S(2)}) collective-permute-start(f32[512,128]{1,0:T(8,128)S(1)} %shard_map.49.refs_3_.refs_6_), channel_id=1, source_target_pairs={{0,4},{4,0},{1,5},{5,1},{2,6},{6,2},{3,7},{7,3},{8,12},{12,8},{9,1... | collective-permute-start | bytes 786440 | tf_op jit(solution)/shard_map/ppermute | solution.py:255
  28.2 9.2 %collective-permute-start.12 = (f32[512,128]{1,0:T(8,128)S(1)}, f32[512,128]{1,0:T(8,128)S(1)}, u32[]{:S(2)}, u32[]{:S(2)}) collective-permute-start(f32[512,128]{1,0:T(8,128)S(1)} %shard_map.53.refs_3_.refs_6_), channel_id=1, source_target_pairs={{0,124},{4,8},{8,4},{12,16},{16,12},{20,24},{24,20},{28,32},{32,28... | collective-permute-start | bytes 786440 | tf_op jit(solution)/shard_map/ppermute | solution.py:254
  29.8 7.7 %collective-permute-start.13 = (f32[512,128]{1,0:T(8,128)S(1)}, f32[512,128]{1,0:T(8,128)S(1)}, u32[]{:S(2)}, u32[]{:S(2)}) collective-permute-start(f32[512,128]{1,0:T(8,128)S(1)} %shard_map.53.refs_3_.refs_6_), channel_id=1, source_target_pairs={{0,4},{4,0},{1,5},{5,1},{2,6},{6,2},{3,7},{7,3},{8,12},{12,8},{9,1... | collective-permute-start | bytes 786440 | tf_op jit(solution)/shard_map/ppermute | solution.py:255
  32.6 9.2 %collective-permute-start.6 = (f32[512,128]{1,0:T(8,128)S(1)}, f32[512,128]{1,0:T(8,128)S(1)}, u32[]{:S(2)}, u32[]{:S(2)}) collective-permute-start(f32[512,128]{1,0:T(8,128)S(1)} %shard_map.50.refs_3_), channel_id=1, source_target_pairs={{0,124},{4,8},{8,4},{12,16},{16,12},{20,24},{24,20},{28,32},{32,28... | collective-permute-start | bytes 786440 | tf_op jit(solution)/shard_map/ppermute | solution.py:254
  37.4 4.4 %collective-permute-start.7 = (f32[512,128]{1,0:T(8,128)S(1)}, f32[512,128]{1,0:T(8,128)S(1)}, u32[]{:S(2)}, u32[]{:S(2)}) collective-permute-start(f32[512,128]{1,0:T(8,128)S(1)} %shard_map.50.refs_3_), channel_id=1, source_target_pairs={{0,4},{4,0},{1,5},{5,1},{2,6},{6,2},{3,7},{7,3},{8,12},{12,8},{9,1... | collective-permute-start | bytes 786440 | tf_op jit(solution)/shard_map/ppermute | solution.py:255
  38.7 9.2 %collective-permute-start.14 = (f32[512,128]{1,0:T(8,128)S(1)}, f32[512,128]{1,0:T(8,128)S(1)}, u32[]{:S(2)}, u32[]{:S(2)}) collective-permute-start(f32[512,128]{1,0:T(8,128)S(1)} %shard_map.54.refs_3_), channel_id=1, source_target_pairs={{0,124},{4,8},{8,4},{12,16},{16,12},{20,24},{24,20},{28,32},{32,28... | collective-permute-start | bytes 786440 | tf_op jit(solution)/shard_map/ppermute | solution.py:254
  40.3 7.7 %collective-permute-start.15 = (f32[512,128]{1,0:T(8,128)S(1)}, f32[512,128]{1,0:T(8,128)S(1)}, u32[]{:S(2)}, u32[]{:S(2)}) collective-permute-start(f32[512,128]{1,0:T(8,128)S(1)} %shard_map.54.refs_3_), channel_id=1, source_target_pairs={{0,4},{4,0},{1,5},{5,1},{2,6},{6,2},{3,7},{7,3},{8,12},{12,8},{9,1... | collective-permute-start | bytes 786440 | tf_op jit(solution)/shard_map/ppermute | solution.py:255
  43.1 11.4 %collective-permute-start.16 = (f32[512,128]{1,0:T(8,128)S(1)}, f32[512,128]{1,0:T(8,128)S(1)}, u32[]{:S(2)}, u32[]{:S(2)}) collective-permute-start(f32[512,128]{1,0:T(8,128)S(1)} %shard_map.51.refs_0_.refs_2_), channel_id=1, source_target_pairs={{0,1},{1,0},{2,3},{3,2},{4,7},{5,6},{6,5},{7,4},{8,9},{9,8},{10,11... | collective-permute-start | bytes 786440 | tf_op jit(solution)/shard_map/ppermute | solution.py:260
  49.2 9.0 %collective-permute-start.17 = (f32[512,128]{1,0:T(8,128)S(1)}, f32[512,128]{1,0:T(8,128)S(1)}, u32[]{:S(2)}, u32[]{:S(2)}) collective-permute-start(f32[512,128]{1,0:T(8,128)S(1)} %shard_map.55.refs_1_.refs_3_), channel_id=1, source_target_pairs={{0,1},{1,0},{2,3},{3,2},{4,7},{5,6},{6,5},{7,4},{8,9},{9,8},{10,11... | collective-permute-start | bytes 786440 | tf_op jit(solution)/shard_map/ppermute | solution.py:262
  51.2 11.3 %collective-permute-start.20 = (f32[512,128]{1,0:T(8,128)S(1)}, f32[512,128]{1,0:T(8,128)S(1)}, u32[]{:S(2)}, u32[]{:S(2)}) collective-permute-start(f32[512,128]{1,0:T(8,128)S(1)} %shard_map.51.refs_0_.refs_2_), channel_id=1, source_target_pairs={{0,3},{1,2},{2,1},{3,0},{4,5},{5,4},{6,7},{7,6},{8,11},{9,10},{10,... | collective-permute-start | bytes 786440 | tf_op jit(solution)/shard_map/ppermute | solution.py:261
  53.8 8.8 %collective-permute-start.21 = (f32[512,128]{1,0:T(8,128)S(1)}, f32[512,128]{1,0:T(8,128)S(1)}, u32[]{:S(2)}, u32[]{:S(2)}) collective-permute-start(f32[512,128]{1,0:T(8,128)S(1)} %shard_map.55.refs_1_.refs_3_), channel_id=1, source_target_pairs={{0,3},{1,2},{2,1},{3,0},{4,5},{5,4},{6,7},{7,6},{8,11},{9,10},{10,... | collective-permute-start | bytes 786440 | tf_op jit(solution)/shard_map/ppermute | solution.py:263
  54.5 10.0 %collective-permute-start.18 = (f32[512,128]{1,0:T(8,128)S(1)}, f32[512,128]{1,0:T(8,128)S(1)}, u32[]{:S(2)}, u32[]{:S(2)}) collective-permute-start(f32[512,128]{1,0:T(8,128)S(1)} %collective-permute-done.16.refs_2_.refs_4_), channel_id=1, source_target_pairs={{0,3},{1,2},{2,1},{3,0},{4,5},{5,4},{6,7},{7,6},{8,11},{9,10},{10,... | collective-permute-start | bytes 786440 | tf_op jit(solution)/shard_map/ppermute | solution.py:264
  58.2 9.0 %collective-permute-start.19 = (f32[512,128]{1,0:T(8,128)S(1)}, f32[512,128]{1,0:T(8,128)S(1)}, u32[]{:S(2)}, u32[]{:S(2)}) collective-permute-start(f32[512,128]{1,0:T(8,128)S(1)} %collective-permute-done.17.refs_3_.refs_5_), channel_id=1, source_target_pairs={{0,3},{1,2},{2,1},{3,0},{4,5},{5,4},{6,7},{7,6},{8,11},{9,10},{10,... | collective-permute-start | bytes 786440 | tf_op jit(solution)/shard_map/ppermute | solution.py:265
  68.2 1.2 %collective-permute-start.22 = (f32[24,128]{1,0:T(8,128)S(1)}, f32[24,128]{1,0:T(8,128)S(1)}, u32[]{:S(2)}, u32[]{:S(2)}) collective-permute-start(f32[24,128]{1,0:T(8,128)S(1)} %shard_map.56), channel_id=1, source_target_pairs={{0,4},{4,0},{1,5},{5,1},{2,6},{6,2},{3,7},{7,3},{8,12},{12,8},{9,1... | collective-permute-start | bytes 36872 | tf_op jit(solution)/shard_map/ppermute | solution.py:269
  (2 other events, 2.2 us)

commit v2 on v1

--- a/solution.py
+++ b/solution.py
@@ -236,7 +236,7 @@
     ring = lax.axis_size("vecs")
     outer = [(i, (i + 1) % count if i % 2 else (i - 1) % count) for i in range(count)]
     inner = [(0, 1), (1, 0)]
-    flips = ((1, 3), (3, 1))
+    flips = ((3, 1), (1, 3))
     early, late = (
         [(k * ring + i, k * ring + (i ^ flips[k][turn])) for k in range(2) for i in range(ring)]
         for turn in range(2)
@@ -266,10 +266,8 @@
     pieces = (a, b, a_early, b_early, a_far, b_far, a_late, b_late)
     flag = core.reshape(1).astype(jnp.int32)
     gram = gram_of(flag, pieces)
-    gram = gram + lax.ppermute(gram, "core", [(0, 1), (1, 0)])
-    chips = lax.axis_size("chip")
     copies = lax.all_to_all(
-        jnp.broadcast_to(gram, (chips, *gram.shape)), "chip", split_axis=0, concat_axis=0, tiled=True
+        jnp.broadcast_to(gram, (count, *gram.shape)), cells, split_axis=0, concat_axis=0, tiled=True
     )
     factor = math.sqrt(float(count * CELLS))
     out = mix(factor, flag, copies, pieces)

time: 83.7 us -> 85.3 us (1.019); the launches traced: 83.4 us -> 84 us
  starting transfers between devices: 39 us -> 35.2 us
  waiting for transfers between devices: 14.8 us -> 18.3 us
  blocking collectives: 12.3 us -> 13.2 us
    ppermute x1, starting transfers between devices: 4.31 us -> 0.01 us  [filtered(): b_far = lax.ppermute(b_early, planes, late)]
    ppermute x1, waiting for transfers between devices: 1.22 us -> 5.1 us  [filtered(): b_early = lax.ppermute(b, planes, early)]
    ppermute x1, starting transfers between devices: 2.53 us -> 0.01 us  [filtered(): a_late = lax.ppermute(a, planes, late)]
    ppermute x1, starting transfers between devices: 2.53 us -> 0.03 us  [filtered(): a_far = lax.ppermute(a_early, planes, late)]
    ppermute x1, starting transfers between devices: 2 us -> 4.12 us  [filtered(): b_early = lax.ppermute(b, planes, early)]
    ppermute x8, waiting for transfers between devices: 7.67 us -> 5.55 us  [filtered(): away = lax.ppermute(cur[h], cells, outer)]
    ppermute x1, starting transfers between devices: 2.1 us -> 4.22 us  [filtered(): a_early = lax.ppermute(a, planes, early)]
    ppermute x1, waiting for transfers between devices: 0.01 us -> 2.02 us  [filtered(): b_late = lax.ppermute(b, planes, late)]
  transfers between devices with their start and end apart: 23 -> 22, of which waited for: 9 -> 9; matrix products, arithmetic and copies ran while one was open for 0% -> 0% of each run, Pallas kernels for 14% -> 14%
where the time goes in v2:
time: 85.3 us; the launch traced here: 84 us
  starting transfers between devices  35.2 us (41%)
  waiting for transfers between devices  18.3 us (21%)
  Pallas kernels  14.1 us (17%)
  blocking collectives  13.2 us (15%)
  local copies, waits for them, and re-layouts  2.24 us (3%)
  between operations  0.91 us (1%)
    ppermute x8, starting transfers between devices, filtered(): away = lax.ppermute(cur[h], cells, outer)  24.8 us
    all_to_all x1, blocking collectives, filtered(): lax.all_to_all(jnp.broadcast_to(gram, (count, *gram.shape)), cells, split...  13.2 us
    pallas_call x8, Pallas kernels, apply_step(): pl.pallas_call(lambda *refs: step_body(first, *refs), in_specs=[pl.BlockS...  10.3 us
    ppermute x8, waiting for transfers between devices, filtered(): away = lax.ppermute(cur[h], cells, outer)  5.55 us
    ppermute x1, waiting for transfers between devices, filtered(): b_early = lax.ppermute(b, planes, early)  5.1 us
    ppermute x1, starting transfers between devices, filtered(): a_early = lax.ppermute(a, planes, early)  4.22 us
    ppermute x1, starting transfers between devices, filtered(): b_early = lax.ppermute(b, planes, early)  4.12 us
    ppermute x1, waiting for transfers between devices, filtered(): a_far = lax.ppermute(a_early, planes, late)  2.81 us
  transfers between devices with their start and end apart: 22, of which 9 were waited for; matrix products, arithmetic and copies ran while one was open for 0% of the time, Pallas kernels for 14%

profile of v2, /device:TPU:0, one launch (start us, length us, event | category | flops | bytes accessed | tf_op | source)
XLA Modules:
  0.0 84.0 jit_solution(11115485724038888099)
XLA Ops:
  1.1 4.8 %collective-permute-start = (f32[512,128]{1,0:T(8,128)S(1)}, f32[512,128]{1,0:T(8,128)S(1)}, u32[]{:S(2)}, u32[]{:S(2)}) collective-permute-start(f32[512,128]{1,0:T(8,128)S(1)} %bitcast.22), channel_id=1, source_target_pairs={{0,124},{4,8},{8,4},{12,16},{16,12},{20,24},{24,20},{28,32},{32,28... | collective-permute-start | bytes 786440 | tf_op jit(solution)/shard_map/ppermute | solution.py:254
  11.6 4.8 %collective-permute-start.2 = (f32[512,128]{1,0:T(8,128)S(1)}, f32[512,128]{1,0:T(8,128)S(1)}, u32[]{:S(2)}, u32[]{:S(2)}) collective-permute-start(f32[512,128]{1,0:T(8,128)S(1)} %shard_map.48.refs_3_.refs_6_), channel_id=1, source_target_pairs={{0,124},{4,8},{8,4},{12,16},{16,12},{20,24},{24,20},{28,32},{32,28... | collective-permute-start | bytes 786440 | tf_op jit(solution)/shard_map/ppermute | solution.py:254
  17.7 1.5 %collective-permute-start.10 = (f32[512,128]{1,0:T(8,128)S(1)}, f32[512,128]{1,0:T(8,128)S(1)}, u32[]{:S(2)}, u32[]{:S(2)}) collective-permute-start(f32[512,128]{1,0:T(8,128)S(1)} %shard_map.52.refs_3_.refs_6_), channel_id=1, source_target_pairs={{0,124},{4,8},{8,4},{12,16},{16,12},{20,24},{24,20},{28,32},{32,28... | collective-permute-start | bytes 786440 | tf_op jit(solution)/shard_map/ppermute | solution.py:254
  19.3 1.5 %collective-permute-done.2.refs_4_ = f32[512,128]{1,0:T(8,128)S(1)} collective-permute-done((f32[512,128]{1,0:T(8,128)S(1)}, f32[512,128]{1,0:T(8,128)S(1)}, u32[]{:S(2)}, u32[]{:S(2)}) %collective-permute-start.2) | collective-permute-done | bytes 262176 | tf_op jit(solution)/shard_map/ppermute | solution.py:254
  20.8 1.3 %shard_map.49.refs_3_.refs_6_ = f32[512,128]{1,0:T(8,128)S(1)} custom-call(f32[1]{0:T(128)S(6)} %copy.6.refs_0_, f32[64,128]{1,0:T(8,128)S(1)} %bitcast.12, bf16[192,1728]{1,0:T(8,128)(2,1)S(1)} %shard_map.46.refs_2_, f32[512,128]{1,0:T(8,128)S(1)} %shard_map.48.refs_3_.refs_6_, f32[512,128]{1,0:T(8,128)S(1)} %collective-permute-done.2.refs_4_, ...), custom_call_target="tpu_custom_call" | custom-call | tf_op jit(solution)/shard_map/pallas_call | solution.py:109
  22.1 4.8 %collective-permute-start.4 = (f32[512,128]{1,0:T(8,128)S(1)}, f32[512,128]{1,0:T(8,128)S(1)}, u32[]{:S(2)}, u32[]{:S(2)}) collective-permute-start(f32[512,128]{1,0:T(8,128)S(1)} %shard_map.49.refs_3_.refs_6_), channel_id=1, source_target_pairs={{0,124},{4,8},{8,4},{12,16},{16,12},{20,24},{24,20},{28,32},{32,28... | collective-permute-start | bytes 786440 | tf_op jit(solution)/shard_map/ppermute | solution.py:254
  26.9 1.3 %shard_map.53.refs_3_.refs_6_ = f32[512,128]{1,0:T(8,128)S(1)} custom-call(f32[1]{0:T(128)S(6)} %copy.6.refs_0_, f32[64,128]{1,0:T(8,128)S(1)} %bitcast.13, bf16[192,1728]{1,0:T(8,128)(2,1)S(1)} %shard_map.46.refs_2_, f32[512,128]{1,0:T(8,128)S(1)} %shard_map.52.refs_3_.refs_6_, f32[512,128]{1,0:T(8,128)S(1)} %collective-permute-done.10.refs_4_, ...), custom_call_target="tpu_custom_call" | custom-call | tf_op jit(solution)/shard_map/pallas_call | solution.py:109
  28.2 1.5 %collective-permute-start.12 = (f32[512,128]{1,0:T(8,128)S(1)}, f32[512,128]{1,0:T(8,128)S(1)}, u32[]{:S(2)}, u32[]{:S(2)}) collective-permute-start(f32[512,128]{1,0:T(8,128)S(1)} %shard_map.53.refs_3_.refs_6_), channel_id=1, source_target_pairs={{0,124},{4,8},{8,4},{12,16},{16,12},{20,24},{24,20},{28,32},{32,28... | collective-permute-start | bytes 786440 | tf_op jit(solution)/shard_map/ppermute | solution.py:254
  29.8 1.5 %collective-permute-done.4.refs_4_ = f32[512,128]{1,0:T(8,128)S(1)} collective-permute-done((f32[512,128]{1,0:T(8,128)S(1)}, f32[512,128]{1,0:T(8,128)S(1)}, u32[]{:S(2)}, u32[]{:S(2)}) %collective-permute-start.4) | collective-permute-done | bytes 262176 | tf_op jit(solution)/shard_map/ppermute | solution.py:254
  31.3 1.3 %shard_map.50.refs_3_ = f32[512,128]{1,0:T(8,128)S(1)} custom-call(f32[1]{0:T(128)S(6)} %copy.6.refs_0_, f32[64,128]{1,0:T(8,128)S(1)} %bitcast.14, bf16[192,1728]{1,0:T(8,128)(2,1)S(1)} %shard_map.46.refs_2_, f32[512,128]{1,0:T(8,128)S(1)} %shard_map.49.refs_3_.refs_6_, f32[512,128]{1,0:T(8,128)S(1)} %collective-permute-done.4.refs_4_, ...), custom_call_target="tpu_custom_call" | custom-call | tf_op jit(solution)/shard_map/pallas_call | solution.py:109
  32.6 4.8 %collective-permute-start.6 = (f32[512,128]{1,0:T(8,128)S(1)}, f32[512,128]{1,0:T(8,128)S(1)}, u32[]{:S(2)}, u32[]{:S(2)}) collective-permute-start(f32[512,128]{1,0:T(8,128)S(1)} %shard_map.50.refs_3_), channel_id=1, source_target_pairs={{0,124},{4,8},{8,4},{12,16},{16,12},{20,24},{24,20},{28,32},{32,28... | collective-permute-start | bytes 786440 | tf_op jit(solution)/shard_map/ppermute | solution.py:254
  37.5 1.3 %shard_map.54.refs_3_ = f32[512,128]{1,0:T(8,128)S(1)} custom-call(f32[1]{0:T(128)S(6)} %copy.6.refs_0_, f32[64,128]{1,0:T(8,128)S(1)} %bitcast.15, bf16[192,1728]{1,0:T(8,128)(2,1)S(1)} %shard_map.46.refs_2_, f32[512,128]{1,0:T(8,128)S(1)} %shard_map.53.refs_3_.refs_6_, f32[512,128]{1,0:T(8,128)S(1)} %collective-permute-done.12.refs_4_, ...), custom_call_target="tpu_custom_call" | custom-call | tf_op jit(solution)/shard_map/pallas_call | solution.py:109
  38.7 1.5 %collective-permute-start.14 = (f32[512,128]{1,0:T(8,128)S(1)}, f32[512,128]{1,0:T(8,128)S(1)}, u32[]{:S(2)}, u32[]{:S(2)}) collective-permute-start(f32[512,128]{1,0:T(8,128)S(1)} %shard_map.54.refs_3_), channel_id=1, source_target_pairs={{0,124},{4,8},{8,4},{12,16},{16,12},{20,24},{24,20},{28,32},{32,28... | collective-permute-start | bytes 786440 | tf_op jit(solution)/shard_map/ppermute | solution.py:254
  40.3 1.5 %collective-permute-done.6.refs_4_ = f32[512,128]{1,0:T(8,128)S(1)} collective-permute-done((f32[512,128]{1,0:T(8,128)S(1)}, f32[512,128]{1,0:T(8,128)S(1)}, u32[]{:S(2)}, u32[]{:S(2)}) %collective-permute-start.6) | collective-permute-done | bytes 262176 | tf_op jit(solution)/shard_map/ppermute | solution.py:254
  43.1 4.2 %collective-permute-start.16 = (f32[512,128]{1,0:T(8,128)S(1)}, f32[512,128]{1,0:T(8,128)S(1)}, u32[]{:S(2)}, u32[]{:S(2)}) collective-permute-start(f32[512,128]{1,0:T(8,128)S(1)} %shard_map.51.refs_0_.refs_2_), channel_id=1, source_target_pairs={{0,3},{1,2},{2,1},{3,0},{4,5},{5,4},{6,7},{7,6},{8,11},{9,10},{10,... | collective-permute-start | bytes 786440 | tf_op jit(solution)/shard_map/ppermute | solution.py:260
  47.9 1.3 %shard_map.55.refs_1_.refs_3_ = f32[512,128]{1,0:T(8,128)S(1)} custom-call(f32[1]{0:T(128)S(6)} %copy.6.refs_0_, f32[64,128]{1,0:T(8,128)S(1)} %bitcast.17, bf16[192,1728]{1,0:T(8,128)(2,1)S(1)} %shard_map.46.refs_2_, f32[512,128]{1,0:T(8,128)S(1)} %shard_map.54.refs_3_, f32[512,128]{1,0:T(8,128)S(1)} %collective-permute-done.14.refs_4_, ...), custom_call_target="tpu_custom_call" | custom-call | tf_op jit(solution)/shard_map/pallas_call | solution.py:109
  49.2 4.1 %collective-permute-start.17 = (f32[512,128]{1,0:T(8,128)S(1)}, f32[512,128]{1,0:T(8,128)S(1)}, u32[]{:S(2)}, u32[]{:S(2)}) collective-permute-start(f32[512,128]{1,0:T(8,128)S(1)} %shard_map.55.refs_1_.refs_3_), channel_id=1, source_target_pairs={{0,3},{1,2},{2,1},{3,0},{4,5},{5,4},{6,7},{7,6},{8,11},{9,10},{10,... | collective-permute-start | bytes 786440 | tf_op jit(solution)/shard_map/ppermute | solution.py:262
  53.4 2.0 %collective-permute-start.21 = (f32[512,128]{1,0:T(8,128)S(1)}, f32[512,128]{1,0:T(8,128)S(1)}, u32[]{:S(2)}, u32[]{:S(2)}) collective-permute-start(f32[512,128]{1,0:T(8,128)S(1)} %shard_map.55.refs_1_.refs_3_), channel_id=1, source_target_pairs={{0,1},{1,0},{2,3},{3,2},{4,7},{5,6},{6,5},{7,4},{8,9},{9,8},{10,11... | collective-permute-start | bytes 786440 | tf_op jit(solution)/shard_map/ppermute | solution.py:263
  55.4 5.1 %collective-permute-done.17.refs_3_.refs_5_ = f32[512,128]{1,0:T(8,128)S(1)} collective-permute-done((f32[512,128]{1,0:T(8,128)S(1)}, f32[512,128]{1,0:T(8,128)S(1)}, u32[]{:S(2)}, u32[]{:S(2)}) %collective-permute-start.17) | collective-permute-done | bytes 262176 | tf_op jit(solution)/shard_map/ppermute | solution.py:262
  60.5 2.0 %collective-permute-done.21.refs_7_.refs_9_ = f32[512,128]{1,0:T(8,128)S(1)} collective-permute-done((f32[512,128]{1,0:T(8,128)S(1)}, f32[512,128]{1,0:T(8,128)S(1)}, u32[]{:S(2)}, u32[]{:S(2)}) %collective-permute-start.21) | collective-permute-done | bytes 262176 | tf_op jit(solution)/shard_map/ppermute | solution.py:263
  62.5 2.8 %collective-permute-done.18.refs_4_.refs_6_ = f32[512,128]{1,0:T(8,128)S(1)} collective-permute-done((f32[512,128]{1,0:T(8,128)S(1)}, f32[512,128]{1,0:T(8,128)S(1)}, u32[]{:S(2)}, u32[]{:S(2)}) %collective-permute-start.18) | collective-permute-done | bytes 262176 | tf_op jit(solution)/shard_map/ppermute | solution.py:264
  65.4 2.8 %collective-permute-done.19.refs_5_.refs_7_ = f32[512,128]{1,0:T(8,128)S(1)} collective-permute-done((f32[512,128]{1,0:T(8,128)S(1)}, f32[512,128]{1,0:T(8,128)S(1)}, u32[]{:S(2)}, u32[]{:S(2)}) %collective-permute-start.19) | collective-permute-done | bytes 262176 | tf_op jit(solution)/shard_map/ppermute | solution.py:265
  69.1 13.2 %all_to_all.5.refs_1_ = f32[32,24,128]{2,1,0:T(8,128)S(1)} all-to-all(f32[32,24,128]{2,1,0:T(8,128)S(1)} %broadcast_in_dim.3), channel_id=1, replica_groups=mesh['chip'=16,'core'=2,'vecs'=4] {'chip','core'}, dimensions={0} | all-to-all | bytes 786432 | tf_op jit(solution)/shard_map/all_to_all | solution.py:269
  82.3 1.5 %shard_map.57 = f32[1024,128]{1,0:T(8,128)} custom-call(s32[1]{0:T(128)} %bitcast.flag.refs_0_, f32[32,24,128]{2,1,0:T(8,128)S(1)} %all_to_all.5.refs_1_, f32[512,128]{1,0:T(8,128)S(1)} %shard_map.51.refs_0_.refs_2_, f32[512,128]{1,0:T(8,128)S(1)} %shard_map.55.refs_1_.refs_3_, f32[512,128]{1,0:T(8,128)S(1)} %collective-permute-done.16.refs_2_.refs_4_, ...), custom_call_target="tpu_custom_call" | custom-call | tf_op jit(solution)/shard_map/pallas_call | solution.py:220
  (41 shorter events, 10.3 us)
Async XLA Ops:
  1.1 9.2 %collective-permute-start = (f32[512,128]{1,0:T(8,128)S(1)}, f32[512,128]{1,0:T(8,128)S(1)}, u32[]{:S(2)}, u32[]{:S(2)}) collective-permute-start(f32[512,128]{1,0:T(8,128)S(1)} %bitcast.22), channel_id=1, source_target_pairs={{0,124},{4,8},{8,4},{12,16},{16,12},{20,24},{24,20},{28,32},{32,28... | collective-permute-start | bytes 786440 | tf_op jit(solution)/shard_map/ppermute | solution.py:254
  5.9 4.4 %collective-permute-start.1 = (f32[512,128]{1,0:T(8,128)S(1)}, f32[512,128]{1,0:T(8,128)S(1)}, u32[]{:S(2)}, u32[]{:S(2)}) collective-permute-start(f32[512,128]{1,0:T(8,128)S(1)} %bitcast.23), channel_id=1, source_target_pairs={{0,4},{4,0},{1,5},{5,1},{2,6},{6,2},{3,7},{7,3},{8,12},{12,8},{9,1... | collective-permute-start | bytes 786440 | tf_op jit(solution)/shard_map/ppermute | solution.py:255
  6.0 10.5 %collective-permute-start.8 = (f32[512,128]{1,0:T(8,128)S(1)}, f32[512,128]{1,0:T(8,128)S(1)}, u32[]{:S(2)}, u32[]{:S(2)}) collective-permute-start(f32[512,128]{1,0:T(8,128)S(1)} %bitcast.18), channel_id=1, source_target_pairs={{0,124},{4,8},{8,4},{12,16},{16,12},{20,24},{24,20},{28,32},{32,28... | collective-permute-start | bytes 786440 | tf_op jit(solution)/shard_map/ppermute | solution.py:254
  6.9 9.6 %collective-permute-start.9 = (f32[512,128]{1,0:T(8,128)S(1)}, f32[512,128]{1,0:T(8,128)S(1)}, u32[]{:S(2)}, u32[]{:S(2)}) collective-permute-start(f32[512,128]{1,0:T(8,128)S(1)} %bitcast.19), channel_id=1, source_target_pairs={{0,4},{4,0},{1,5},{5,1},{2,6},{6,2},{3,7},{7,3},{8,12},{12,8},{9,1... | collective-permute-start | bytes 786440 | tf_op jit(solution)/shard_map/ppermute | solution.py:255
  7.6 1.2 %copy-start.1 = (f32[27,64,64]{2,1,0:T(8,128)S(1)}, f32[27,64,64]{2,1,0:T(8,128)}, u32[]{:S(2)}) copy-start(f32[27,64,64]{2,1,0:T(8,128)} %hop.1) | copy-start | bytes 1327108
  8.8 1.5 %copy-start = (f32[64,1,128]{2,1,0:T(1,128)S(1)}, f32[64,1,128]{2,1,0:T(1,128)}, u32[]{:S(2)}) copy-start(f32[64,1,128]{2,1,0:T(1,128)} %param.5) | copy-start | bytes 98308
  11.6 9.2 %collective-permute-start.2 = (f32[512,128]{1,0:T(8,128)S(1)}, f32[512,128]{1,0:T(8,128)S(1)}, u32[]{:S(2)}, u32[]{:S(2)}) collective-permute-start(f32[512,128]{1,0:T(8,128)S(1)} %shard_map.48.refs_3_.refs_6_), channel_id=1, source_target_pairs={{0,124},{4,8},{8,4},{12,16},{16,12},{20,24},{24,20},{28,32},{32,28... | collective-permute-start | bytes 786440 | tf_op jit(solution)/shard_map/ppermute | solution.py:254
  16.4 4.4 %collective-permute-start.3 = (f32[512,128]{1,0:T(8,128)S(1)}, f32[512,128]{1,0:T(8,128)S(1)}, u32[]{:S(2)}, u32[]{:S(2)}) collective-permute-start(f32[512,128]{1,0:T(8,128)S(1)} %shard_map.48.refs_3_.refs_6_), channel_id=1, source_target_pairs={{0,4},{4,0},{1,5},{5,1},{2,6},{6,2},{3,7},{7,3},{8,12},{12,8},{9,1... | collective-permute-start | bytes 786440 | tf_op jit(solution)/shard_map/ppermute | solution.py:255
  17.7 9.2 %collective-permute-start.10 = (f32[512,128]{1,0:T(8,128)S(1)}, f32[512,128]{1,0:T(8,128)S(1)}, u32[]{:S(2)}, u32[]{:S(2)}) collective-permute-start(f32[512,128]{1,0:T(8,128)S(1)} %shard_map.52.refs_3_.refs_6_), channel_id=1, source_target_pairs={{0,124},{4,8},{8,4},{12,16},{16,12},{20,24},{24,20},{28,32},{32,28... | collective-permute-start | bytes 786440 | tf_op jit(solution)/shard_map/ppermute | solution.py:254
  19.2 7.7 %collective-permute-start.11 = (f32[512,128]{1,0:T(8,128)S(1)}, f32[512,128]{1,0:T(8,128)S(1)}, u32[]{:S(2)}, u32[]{:S(2)}) collective-permute-start(f32[512,128]{1,0:T(8,128)S(1)} %shard_map.52.refs_3_.refs_6_), channel_id=1, source_target_pairs={{0,4},{4,0},{1,5},{5,1},{2,6},{6,2},{3,7},{7,3},{8,12},{12,8},{9,1... | collective-permute-start | bytes 786440 | tf_op jit(solution)/shard_map/ppermute | solution.py:255
  22.1 9.2 %collective-permute-start.4 = (f32[512,128]{1,0:T(8,128)S(1)}, f32[512,128]{1,0:T(8,128)S(1)}, u32[]{:S(2)}, u32[]{:S(2)}) collective-permute-start(f32[512,128]{1,0:T(8,128)S(1)} %shard_map.49.refs_3_.refs_6_), channel_id=1, source_target_pairs={{0,124},{4,8},{8,4},{12,16},{16,12},{20,24},{24,20},{28,32},{32,28... | collective-permute-start | bytes 786440 | tf_op jit(solution)/shard_map/ppermute | solution.py:254
  26.9 4.4 %collective-permute-start.5 = (f32[512,128]{1,0:T(8,128)S(1)}, f32[512,128]{1,0:T(8,128)S(1)}, u32[]{:S(2)}, u32[]{:S(2)}) collective-permute-start(f32[512,128]{1,0:T(8,128)S(1)} %shard_map.49.refs_3_.refs_6_), channel_id=1, source_target_pairs={{0,4},{4,0},{1,5},{5,1},{2,6},{6,2},{3,7},{7,3},{8,12},{12,8},{9,1... | collective-permute-start | bytes 786440 | tf_op jit(solution)/shard_map/ppermute | solution.py:255
  28.2 9.2 %collective-permute-start.12 = (f32[512,128]{1,0:T(8,128)S(1)}, f32[512,128]{1,0:T(8,128)S(1)}, u32[]{:S(2)}, u32[]{:S(2)}) collective-permute-start(f32[512,128]{1,0:T(8,128)S(1)} %shard_map.53.refs_3_.refs_6_), channel_id=1, source_target_pairs={{0,124},{4,8},{8,4},{12,16},{16,12},{20,24},{24,20},{28,32},{32,28... | collective-permute-start | bytes 786440 | tf_op jit(solution)/shard_map/ppermute | solution.py:254
  29.8 7.7 %collective-permute-start.13 = (f32[512,128]{1,0:T(8,128)S(1)}, f32[512,128]{1,0:T(8,128)S(1)}, u32[]{:S(2)}, u32[]{:S(2)}) collective-permute-start(f32[512,128]{1,0:T(8,128)S(1)} %shard_map.53.refs_3_.refs_6_), channel_id=1, source_target_pairs={{0,4},{4,0},{1,5},{5,1},{2,6},{6,2},{3,7},{7,3},{8,12},{12,8},{9,1... | collective-permute-start | bytes 786440 | tf_op jit(solution)/shard_map/ppermute | solution.py:255
  32.6 9.2 %collective-permute-start.6 = (f32[512,128]{1,0:T(8,128)S(1)}, f32[512,128]{1,0:T(8,128)S(1)}, u32[]{:S(2)}, u32[]{:S(2)}) collective-permute-start(f32[512,128]{1,0:T(8,128)S(1)} %shard_map.50.refs_3_), channel_id=1, source_target_pairs={{0,124},{4,8},{8,4},{12,16},{16,12},{20,24},{24,20},{28,32},{32,28... | collective-permute-start | bytes 786440 | tf_op jit(solution)/shard_map/ppermute | solution.py:254
  37.4 4.4 %collective-permute-start.7 = (f32[512,128]{1,0:T(8,128)S(1)}, f32[512,128]{1,0:T(8,128)S(1)}, u32[]{:S(2)}, u32[]{:S(2)}) collective-permute-start(f32[512,128]{1,0:T(8,128)S(1)} %shard_map.50.refs_3_), channel_id=1, source_target_pairs={{0,4},{4,0},{1,5},{5,1},{2,6},{6,2},{3,7},{7,3},{8,12},{12,8},{9,1... | collective-permute-start | bytes 786440 | tf_op jit(solution)/shard_map/ppermute | solution.py:255
  38.7 9.2 %collective-permute-start.14 = (f32[512,128]{1,0:T(8,128)S(1)}, f32[512,128]{1,0:T(8,128)S(1)}, u32[]{:S(2)}, u32[]{:S(2)}) collective-permute-start(f32[512,128]{1,0:T(8,128)S(1)} %shard_map.54.refs_3_), channel_id=1, source_target_pairs={{0,124},{4,8},{8,4},{12,16},{16,12},{20,24},{24,20},{28,32},{32,28... | collective-permute-start | bytes 786440 | tf_op jit(solution)/shard_map/ppermute | solution.py:254
  40.3 7.7 %collective-permute-start.15 = (f32[512,128]{1,0:T(8,128)S(1)}, f32[512,128]{1,0:T(8,128)S(1)}, u32[]{:S(2)}, u32[]{:S(2)}) collective-permute-start(f32[512,128]{1,0:T(8,128)S(1)} %shard_map.54.refs_3_), channel_id=1, source_target_pairs={{0,4},{4,0},{1,5},{5,1},{2,6},{6,2},{3,7},{7,3},{8,12},{12,8},{9,1... | collective-permute-start | bytes 786440 | tf_op jit(solution)/shard_map/ppermute | solution.py:255
  43.1 12.3 %collective-permute-start.16 = (f32[512,128]{1,0:T(8,128)S(1)}, f32[512,128]{1,0:T(8,128)S(1)}, u32[]{:S(2)}, u32[]{:S(2)}) collective-permute-start(f32[512,128]{1,0:T(8,128)S(1)} %shard_map.51.refs_0_.refs_2_), channel_id=1, source_target_pairs={{0,3},{1,2},{2,1},{3,0},{4,5},{5,4},{6,7},{7,6},{8,11},{9,10},{10,... | collective-permute-start | bytes 786440 | tf_op jit(solution)/shard_map/ppermute | solution.py:260
  49.2 11.3 %collective-permute-start.17 = (f32[512,128]{1,0:T(8,128)S(1)}, f32[512,128]{1,0:T(8,128)S(1)}, u32[]{:S(2)}, u32[]{:S(2)}) collective-permute-start(f32[512,128]{1,0:T(8,128)S(1)} %shard_map.55.refs_1_.refs_3_), channel_id=1, source_target_pairs={{0,3},{1,2},{2,1},{3,0},{4,5},{5,4},{6,7},{7,6},{8,11},{9,10},{10,... | collective-permute-start | bytes 786440 | tf_op jit(solution)/shard_map/ppermute | solution.py:262
  53.4 7.2 %collective-permute-start.20 = (f32[512,128]{1,0:T(8,128)S(1)}, f32[512,128]{1,0:T(8,128)S(1)}, u32[]{:S(2)}, u32[]{:S(2)}) collective-permute-start(f32[512,128]{1,0:T(8,128)S(1)} %shard_map.51.refs_0_.refs_2_), channel_id=1, source_target_pairs={{0,1},{1,0},{2,3},{3,2},{4,7},{5,6},{6,5},{7,4},{8,9},{9,8},{10,11... | collective-permute-start | bytes 786440 | tf_op jit(solution)/shard_map/ppermute | solution.py:261
  53.4 9.2 %collective-permute-start.21 = (f32[512,128]{1,0:T(8,128)S(1)}, f32[512,128]{1,0:T(8,128)S(1)}, u32[]{:S(2)}, u32[]{:S(2)}) collective-permute-start(f32[512,128]{1,0:T(8,128)S(1)} %shard_map.55.refs_1_.refs_3_), channel_id=1, source_target_pairs={{0,1},{1,0},{2,3},{3,2},{4,7},{5,6},{6,5},{7,4},{8,9},{9,8},{10,11... | collective-permute-start | bytes 786440 | tf_op jit(solution)/shard_map/ppermute | solution.py:263
  55.4 10.0 %collective-permute-start.18 = (f32[512,128]{1,0:T(8,128)S(1)}, f32[512,128]{1,0:T(8,128)S(1)}, u32[]{:S(2)}, u32[]{:S(2)}) collective-permute-start(f32[512,128]{1,0:T(8,128)S(1)} %collective-permute-done.16.refs_2_.refs_4_), channel_id=1, source_target_pairs={{0,1},{1,0},{2,3},{3,2},{4,7},{5,6},{6,5},{7,4},{8,9},{9,8},{10,11... | collective-permute-start | bytes 786440 | tf_op jit(solution)/shard_map/ppermute | solution.py:264
  60.5 7.6 %collective-permute-start.19 = (f32[512,128]{1,0:T(8,128)S(1)}, f32[512,128]{1,0:T(8,128)S(1)}, u32[]{:S(2)}, u32[]{:S(2)}) collective-permute-start(f32[512,128]{1,0:T(8,128)S(1)} %collective-permute-done.17.refs_3_.refs_5_), channel_id=1, source_target_pairs={{0,1},{1,0},{2,3},{3,2},{4,7},{5,6},{6,5},{7,4},{8,9},{9,8},{10,11... | collective-permute-start | bytes 786440 | tf_op jit(solution)/shard_map/ppermute | solution.py:265
  (1 other events, 1.0 us)
